TPU v7x, 256 devices: a whole 4x4x8 slice. The times are simulated.
256 devices in a mesh: pipe: 8 (over x, z_lo), tensor: 4 (over y), expert: 8 (over z_hi, core).
Axes of the slice: x: 4, y: 4, z: 8 (z_hi: 4, z_lo: 2; z = z_hi * 2 + z_lo), core: 2. Of those that a mesh axis runs over, the one named last changes fastest.
Arguments:
- tokens: bfloat16 [2, 512, 4096], P(None, 'expert'), may hold values from -6 to 6
- gains: float32 [8, 4096], P('pipe'), may hold values from 0.1 to 1.9
- route_ids: int32 [8, 2, 512, 2], P('pipe', None, 'expert'), may hold values from 0 to 7, all different within a row
- route_weights: float32 [8, 2, 512, 2], P('pipe', None, 'expert'), may hold values from 0.2 to 1
- picks: int32 [8, 2, 8, 64], P('pipe', None, 'expert'), may hold values from 0 to 63, each once within a row
- w_gate: bfloat16 [8, 8, 4096, 1536], P('pipe', 'expert', None, 'tensor'), may hold values from -0.09375 to 0.09375
- w_up: bfloat16 [8, 8, 4096, 1536], P('pipe', 'expert', None, 'tensor'), may hold values from -0.09375 to 0.09375
- w_down: bfloat16 [8, 8, 1536, 4096], P('pipe', 'expert', 'tensor'), may hold values from -0.15625 to 0.15625
Outputs:
- streams: bfloat16 [8, 2, 512, 4096], P('pipe', None, 'expert', 'tensor')
Inputs may be any that keep to these rules, and one draw needn't show every extreme that they name: `route_ids`: each token names 2 different experts; every expert is named by some token. `picks`: for every layer, micro-batch and block of 64 tokens, a permutation of 0 to 63.
All inputs are finite; a program needn't handle non-finite values.
Results may differ from a plain program's by a relative error of at most 0.025.
Values may be sent and summed in bfloat16 or wider, within the bound.
No kernel may reach another device: no remote copies, remote signals or barrier semaphores. Data moves between devices by JAX's collectives and lax.ppermute only.
A program may use at most 64 MiB of HBM per device.

v0:
```python
import functools

import jax
import jax.numpy as jnp
from jax import lax
from jax.experimental import pallas as pl
from jax.experimental.pallas import tpu as pltpu
from jax.sharding import PartitionSpec as P

epsilon = 1e-06
bf16 = jnp.bfloat16
f32 = jnp.float32
i32 = jnp.int32
SMEM = pl.BlockSpec(memory_space=pltpu.SMEM)
VMEM = pl.BlockSpec(memory_space=pltpu.VMEM)
HBM = pl.BlockSpec(memory_space=pltpu.HBM)
CHIP_SHIFTS = (2, 1, 3)
RANK_SHIFTS = (2, 1, 3)


def kernel_call(body, name, in_specs, out_shapes, mib, scratch=(), flops=0, moved=0):
    return pl.pallas_call(
        body,
        name=name,
        in_specs=in_specs,
        out_specs=jax.tree.map(lambda _: VMEM, out_shapes),
        out_shape=out_shapes,
        scratch_shapes=list(scratch),
        compiler_params=pltpu.CompilerParams(vmem_limit_bytes=mib << 20),
        cost_estimate=pl.CostEstimate(flops=flops, bytes_accessed=moved, transcendentals=0),
    )


def shifted(block, axis, distance):
    size = lax.axis_size(axis)
    return lax.ppermute(block, axis, [(i, (i + distance) % size) for i in range(size)])


def core_swap(block):
    size = lax.axis_size("expert")
    return lax.ppermute(block, "expert", [(i, i ^ 1) for i in range(size)])


def onward(block, chips_on):
    sections, groups = lax.axis_size("pipe"), lax.axis_size("expert")
    route = [
        (s * groups + e, ((s + 1) % sections) * groups + (e + 2 * chips_on) % groups)
        for s in range(sections)
        for e in range(groups)
    ]
    return lax.ppermute(block, ("pipe", "expert"), route)


def tables_kernel(sizes, where, info, place, high, low):
    chips, ranks, quarter, capacity = sizes
    tokens = info.shape[3]
    rows = place.shape[2]
    per_pair = ranks * capacity
    chip, core = where[0].astype(f32), where[1].astype(f32)
    across = lax.broadcasted_iota(i32, (tokens, tokens), 1)
    down = lax.broadcasted_iota(i32, (tokens, tokens), 0)
    across_f, down_f = across.astype(f32), down.astype(f32)
    spots = lax.broadcasted_iota(i32, (tokens, rows), 1).astype(f32)

    def column(row):
        return jnp.sum(jnp.where(across == down, row, 0.0), axis=1, keepdims=True)

    for micro in range(info.shape[0]):
        for home in range(2):
            known = info[micro, home]
            id_rows = [known[k : k + 1] for k in range(2)]
            order = known[2:3]
            place_col = jnp.sum(jnp.where(order == down_f, across_f, 0.0), axis=1, keepdims=True)
            place_row = jnp.sum(jnp.where(column(order) == across_f, down_f, 0.0), axis=0, keepdims=True)
            part_col = jnp.floor(place_col * (1.0 / quarter))
            part_row = jnp.floor(place_row * (1.0 / quarter))
            ahead = (part_col == part_row) & (place_row < place_col)
            span = slice(home * tokens, (home + 1) * tokens)
            hot = jnp.zeros((tokens, rows), f32)
            mixed = jnp.zeros((tokens, rows), f32)
            for k in range(2):
                ids = column(id_rows[k])
                same = jnp.where(id_rows[0] == ids, 1.0, 0.0) + jnp.where(id_rows[1] == ids, 1.0, 0.0)
                slot = jnp.sum(jnp.where(ahead, same, 0.0), axis=1, keepdims=True)
                its_chip = jnp.floor(ids * 0.5)
                away = its_chip - chip
                away = jnp.where(away < 0.0, away + chips, away)
                row = away * (2 * per_pair) + home * per_pair + part_col * capacity + slot
                row = jnp.where((slot < capacity) & (ids - 2.0 * its_chip == core), row, -1.0)
                hit = row == spots
                hot = jnp.where(hit, 1.0, hot)
                mixed = jnp.where(hit, column(known[3 + k : 4 + k]), mixed)
            top = mixed.astype(bf16)
            place[micro, span] = hot.astype(bf16)
            high[micro, span] = top
            low[micro, span] = (mixed - top.astype(f32)).astype(bf16)


def dispatch_kernel(which, place, stream, *outs):
    rows = lax.dot_general(
        place[which[0]], stream[...], (((0,), (0,)), ((), ())), preferred_element_type=f32
    )
    count = outs[0].shape[0]
    for k, out in enumerate(outs):
        out[...] = rows[k * count : (k + 1) * count].astype(bf16)


def combine_kernel(which, high, low, *refs):
    *blocks, out = refs
    rows = jnp.concatenate([block[...].astype(f32) for block in blocks]).astype(bf16)
    update = jnp.dot(high[which[0]], rows, preferred_element_type=f32)
    out[...] = update + jnp.dot(low[which[0]], rows, preferred_element_type=f32)


def gate_up_kernel(shifts, last, model_width, rank, gains, w_gate, w_up, *refs):
    count = len(shifts)
    slices = refs[:count]
    refs = refs[count:]
    if last:
        gate_in, up_in, squares_in, hidden, gate_buf, up_buf, sems = refs
    else:
        gate_out, up_out, squares_out, gate_buf, up_buf, sems = refs
    width = slices[0].shape[1]
    ranks = w_gate.shape[0] // width
    copies = []
    for i, k in enumerate(shifts):
        start = lax.rem(rank[0] + (ranks - k), ranks) * width
        pair = [
            pltpu.make_async_copy(src.at[pl.ds(start, width)], buf.at[i], sems.at[i, j])
            for j, (src, buf) in enumerate(((w_gate, gate_buf), (w_up, up_buf)))
        ]
        for copy in pair:
            copy.start()
        copies.append(pair)
    if last:
        gate, up, squares = gate_in[...], up_in[...], squares_in[:, :1]
    else:
        gate, up, squares = 0.0, 0.0, 0.0
    for i, k in enumerate(shifts):
        wide = slices[i][...].astype(f32)
        squares = squares + jnp.sum(wide * wide, axis=1, keepdims=True)
        scaled = (wide * gains[k : k + 1]).astype(bf16)
        copies[i][0].wait()
        gate = gate + jnp.dot(scaled, gate_buf[i], preferred_element_type=f32)
        copies[i][1].wait()
        up = up + jnp.dot(scaled, up_buf[i], preferred_element_type=f32)
    if last:
        inv_rms = lax.rsqrt(squares * (1.0 / model_width) + epsilon)
        gate = gate * inv_rms
        hidden[...] = (gate / (1.0 + jnp.exp(-gate)) * (up * inv_rms)).astype(bf16)
    else:
        gate_out[...] = gate
        up_out[...] = up
        squares_out[...] = jnp.broadcast_to(squares, squares_out.shape)


def down_kernel(last, count, *refs):
    parts, matrices, refs = refs[:count], refs[count : 2 * count], refs[2 * count :]
    if last:
        before, *outs, buf, sems = refs
    else:
        out, buf, sems = refs
    copies = [pltpu.make_async_copy(matrices[i], buf.at[i], sems.at[i]) for i in range(count)]
    for copy in copies:
        copy.start()
    total = before[...] if last else 0.0
    for i in range(count):
        copies[i].wait()
        total = total + jnp.dot(parts[i][...], buf[i], preferred_element_type=f32)
    if last:
        size = outs[0].shape[0]
        for k, piece in enumerate(outs):
            piece[...] = total[k * size : (k + 1) * size].astype(bf16)
    else:
        out[...] = total


def local(tokens, gains, route_ids, route_weights, picks, w_gate, w_up, w_down):
    micro_count, local_tokens, model_width = tokens.shape
    route_count = route_ids.shape[3]
    ranks = lax.axis_size("tensor")
    groups = lax.axis_size("expert")
    sections = lax.axis_size("pipe")
    chips = groups // 2
    quarter = local_tokens // ranks
    capacity = 4 * quarter * route_count // (3 * groups)
    width = model_width // ranks
    hidden_width = w_gate.shape[3]
    per_chip = 2 * ranks * capacity
    rows = chips * per_chip
    section = lax.axis_index("pipe")
    rank = lax.axis_index("tensor")
    group = lax.axis_index("expert")
    chip, core = group // 2, group % 2
    gate_matrix, up_matrix, down_matrix = w_gate[0, 0], w_up[0, 0], w_down[0, 0]

    def slice_at(value, index, dim):
        return lax.dynamic_slice_in_dim(value, ((index + ranks) % ranks) * width, width, dim)

    def by_core(mine, guest, dim):
        first = jnp.where(core == 0, mine, guest)
        second = jnp.where(core == 0, guest, mine)
        return jnp.concatenate([first, second], axis=dim)

    def shape(*dims, kind=bf16):
        return jax.ShapeDtypeStruct(dims, kind)

    info = jnp.concatenate(
        [route_ids[0].transpose(0, 2, 1).astype(f32), picks[0].astype(f32), route_weights[0].transpose(0, 2, 1)],
        axis=1,
    )[:, None]
    info = by_core(info, core_swap(info), 1)
    where = jnp.stack([chip, core]).astype(i32)
    table = shape(micro_count, 2 * local_tokens, rows)
    tables = kernel_call(
        functools.partial(tables_kernel, (chips, ranks, quarter, capacity)),
        "tables",
        (SMEM, VMEM),
        (table, table, table),
        8,
    )
    first_place, high, low = tables(where, info)

    own_slice = lax.dynamic_slice_in_dim(tokens, rank * width, width, 2)
    entering = by_core(own_slice, core_swap(own_slice), 1)

    dispatch = kernel_call(
        dispatch_kernel, "dispatch", (SMEM, VMEM, VMEM), (shape(per_chip, width),) * chips, 8, flops=10**9
    )
    combine = kernel_call(
        combine_kernel,
        "combine",
        (SMEM, VMEM, VMEM) + (VMEM,) * chips,
        shape(2 * local_tokens, width, kind=f32),
        8,
        flops=10**9,
    )
    half = (shape(rows, hidden_width, kind=f32),) * 2 + (shape(rows, 128, kind=f32),)
    buffers = [pltpu.VMEM((2, width, hidden_width), bf16)] * 2 + [pltpu.SemaphoreType.DMA((2, 2))]
    early, late = (0, 1), (3, 2)
    gate_up = [
        kernel_call(
            functools.partial(gate_up_kernel, shifts, last, model_width),
            name,
            (SMEM, VMEM, HBM, HBM, VMEM, VMEM) + (VMEM,) * (3 * last),
            shape(rows, hidden_width) if last else half,
            16,
            buffers,
            flops=2 * 10**9,
        )
        for name, shifts, last in (("gate_up_a", early, False), ("gate_up_b", late, True))
    ]
    down_buffers = [pltpu.VMEM((2, hidden_width, width), bf16), pltpu.SemaphoreType.DMA((2,))]
    down = [
        kernel_call(
            functools.partial(down_kernel, last, 2),
            name,
            (VMEM, VMEM, HBM, HBM) + (VMEM,) * last,
            (shape(per_chip, width),) * chips if last else shape(rows, width, kind=f32),
            10,
            down_buffers,
            flops=10**9,
        )
        for name, last in (("down_a", False), ("down_b", True))
    ]

    rank_word = rank.reshape(1).astype(i32)
    gain_parts = jnp.concatenate([slice_at(gains, rank - k, 1) for k in range(ranks)])

    def expert_work(blocks, down_parts, also):
        own = jnp.concatenate(blocks)
        slices = {k: shifted(own, "tensor", k) for k in RANK_SHIFTS}
        slices[0] = own
        weights = (rank_word, gain_parts, gate_matrix, up_matrix)
        partial = gate_up[0](*weights, *(slices[k] for k in early))
        hidden = gate_up[1](*weights, *(slices[k] for k in late), *partial)
        hidden, also = lax.optimization_barrier((hidden, also))
        hiddens = {k: shifted(hidden, "tensor", k) for k in RANK_SHIFTS}
        hiddens[0] = hidden
        total = down[0](*(hiddens[k] for k in early), *(down_parts[k] for k in early))
        return down[1](*(hiddens[k] for k in late), *(down_parts[k] for k in late), total), also

    def to_home(blocks):
        back = {k: shifted(blocks[k], "expert", groups - 2 * k) for k in CHIP_SHIFTS}
        back[0] = blocks[0]
        return [back[k] for k in range(chips)]

    def combined(stream, blocks, which):
        update = combine(which.reshape(1), high, low, *blocks)
        return (stream.astype(f32) + (update + core_swap(update))).astype(bf16)

    def kept(collected, fresh, spot):
        own = lax.dynamic_slice_in_dim(fresh, core * local_tokens, local_tokens)
        return lax.dynamic_update_slice_in_dim(collected, own[None], spot, 0)

    outgoing = dispatch(jnp.zeros(1, i32), first_place, entering[0])
    moved = {k: shifted(outgoing[k], "expert", 2 * k) for k in CHIP_SHIFTS}
    moved[0] = outgoing[0]

    down_parts = {k: shifted(slice_at(down_matrix, rank + k, 1), "tensor", k) for k in RANK_SHIFTS}
    down_parts[0] = slice_at(down_matrix, rank, 1)
    next_info = shifted(info, "pipe", sections - 1)
    place = tables(where, next_info)[0]

    blocks, stream = expert_work([moved[k] for k in range(chips)], down_parts, entering[0])
    fresh = combined(stream, to_home(blocks), jnp.zeros((), i32))
    collected = kept(jnp.zeros((micro_count + 1, local_tokens, width), bf16), fresh, 0)
    fresh = jnp.where(section == sections - 1, entering[1], fresh)

    def tick(index, carry):
        fresh, collected = carry
        unit = index - section
        leaving = jnp.where(section == sections - 1, 1, jnp.clip(unit - 1, 0, micro_count - 1))
        outgoing = dispatch(leaving.reshape(1), place, fresh)
        moved = {k: onward(outgoing[k], k) for k in (*CHIP_SHIFTS, 0)}
        stream = shifted(fresh, "pipe", 1)
        blocks, stream = expert_work([moved[k] for k in range(chips)], down_parts, stream)
        fresh = combined(stream, to_home(blocks), jnp.clip(unit, 0, micro_count - 1))
        return fresh, kept(collected, fresh, jnp.clip(unit, 0, micro_count))

    fresh, collected = lax.fori_loop(1, micro_count + sections - 1, tick, (fresh, collected))
    return collected[None, :micro_count]


def solution(mesh):
    return jax.shard_map(
        local,
        mesh=mesh,
        in_specs=(
            P(None, "expert", None),
            P("pipe", None),
            P("pipe", None, "expert", None),
            P("pipe", None, "expert", None),
            P("pipe", None, "expert", None),
            P("pipe", "expert", None, "tensor"),
            P("pipe", "expert", None, "tensor"),
            P("pipe", "expert", "tensor", None),
        ),
        out_specs=P("pipe", None, "expert", "tensor"),
        check_vma=False,
    )
```

profile of v0, /device:TPU:1, one launch (start us, length us, event | category | flops | bytes accessed | tf_op | source)
XLA Modules:
  0.0 651.4 jit_solution(7894615569456803772)
XLA Ops:
  41.4 33.4 %collective-permute-done.20.refs_0_ = bf16[160,1024]{1,0:T(8,128)(2,1)S(1)} collective-permute-done((bf16[160,1024]{1,0:T(8,128)(2,1)S(1)}, bf16[160,1024]{1,0:T(8,128)(2,1)S(1)}, u32[]{:S(2)}, u32[]{:S(2)}) %collective-permute-start.20) | collective-permute-done | bytes 327712 | tf_op jit(solution)/shard_map/ppermute | solution.py:36
  116.6 533.1 %while.17 = (s32[]{:T(128)}, bf16[128,1024]{1,0:T(8,128)(2,1)}, bf16[3,64,1024]{2,1,0:T(8,128)(2,1)}, s32[]{:T(128)}, pred[]{:T(512)}, /*index=5*/bf16[2,128,160...) while((s32[]{:T(128)}, bf16[128,1024]{1,0:T(8,128)(2,1)}, ...), condition=%wide.region_1.2_spmd, body=%wide.region_0.1_spmd.sunk | while | flops 8000524288 | bytes 42698272 | solution.py:321
  158.7 7.7 %collective-permute-start.11 = (bf16[40,1024]{1,0:T(8,128)(2,1)S(1)}, bf16[40,1024]{1,0:T(8,128)(2,1)S(1)}, u32[]{:S(2)}, u32[]{:S(2)}) collective-permute-start(bf16[40,1024]{1,0:T(8,128)(2,1)S(1)} %get-tuple-element.586), channel_id=1, source_target_pairs={{0,6},{1,7},{2,0},{3,1},{4,2},{5,3},{6,4},{7,5},{8,14},{9,15},{10,... | collective-permute-start | bytes 245768 | tf_op jit(solution)/shard_map/while/body/eval_jaxpr/ppermute | solution.py:36
  168.6 5.8 collective-permute-done.12.refs_2_
  186.8 5.7 collective-permute-start.3
  200.5 7.8 %collective-permute-done.6.refs_1_ = bf16[160,1024]{1,0:T(8,128)(2,1)S(1)} collective-permute-done((bf16[160,1024]{1,0:T(8,128)(2,1)S(1)}, bf16[160,1024]{1,0:T(8,128)(2,1)S(1)}, u32[]{:S(2)}, u32[]{:S(2)}) %collective-permute-start.6) | collective-permute-done | bytes 327712 | tf_op jit(solution)/shard_map/while/body/eval_jaxpr/ppermute | solution.py:36
  226.3 5.7 collective-permute-start.12
  238.7 8.3 %collective-permute-start.14 = (f32[128,1024]{1,0:T(8,128)S(1)}, f32[128,1024]{1,0:T(8,128)S(1)}, u32[]{:S(2)}, u32[]{:S(2)}) collective-permute-start(f32[128,1024]{1,0:T(8,128)S(1)} %combine.10), channel_id=1, source_target_pairs={{0,1},{1,0},{2,3},{3,2},{4,5},{5,4},{6,7},{7,6},{8,9},{9,8},{10,11... | collective-permute-start | bytes 1572872 | tf_op jit(solution)/shard_map/while/body/eval_jaxpr/ppermute | solution.py:41
  266.7 7.0 %collective-permute-done.6.refs_1_ = bf16[160,1024]{1,0:T(8,128)(2,1)S(1)} collective-permute-done((bf16[160,1024]{1,0:T(8,128)(2,1)S(1)}, bf16[160,1024]{1,0:T(8,128)(2,1)S(1)}, u32[]{:S(2)}, u32[]{:S(2)}) %collective-permute-start.6) | collective-permute-done | bytes 327712 | tf_op jit(solution)/shard_map/while/body/eval_jaxpr/ppermute | solution.py:36
  306.1 8.5 %collective-permute-start.14 = (f32[128,1024]{1,0:T(8,128)S(1)}, f32[128,1024]{1,0:T(8,128)S(1)}, u32[]{:S(2)}, u32[]{:S(2)}) collective-permute-start(f32[128,1024]{1,0:T(8,128)S(1)} %combine.10), channel_id=1, source_target_pairs={{0,1},{1,0},{2,3},{3,2},{4,5},{5,4},{6,7},{7,6},{8,9},{9,8},{10,11... | collective-permute-start | bytes 1572872 | tf_op jit(solution)/shard_map/while/body/eval_jaxpr/ppermute | solution.py:41
  333.4 6.2 collective-permute-done.6.refs_1_
  356.7 7.3 %collective-permute-start.11 = (bf16[40,1024]{1,0:T(8,128)(2,1)S(1)}, bf16[40,1024]{1,0:T(8,128)(2,1)S(1)}, u32[]{:S(2)}, u32[]{:S(2)}) collective-permute-start(bf16[40,1024]{1,0:T(8,128)(2,1)S(1)} %get-tuple-element.586), channel_id=1, source_target_pairs={{0,6},{1,7},{2,0},{3,1},{4,2},{5,3},{6,4},{7,5},{8,14},{9,15},{10,... | collective-permute-start | bytes 245768 | tf_op jit(solution)/shard_map/while/body/eval_jaxpr/ppermute | solution.py:36
  366.1 5.8 collective-permute-done.12.refs_2_
  373.3 8.6 %collective-permute-start.14 = (f32[128,1024]{1,0:T(8,128)S(1)}, f32[128,1024]{1,0:T(8,128)S(1)}, u32[]{:S(2)}, u32[]{:S(2)}) collective-permute-start(f32[128,1024]{1,0:T(8,128)S(1)} %combine.10), channel_id=1, source_target_pairs={{0,1},{1,0},{2,3},{3,2},{4,5},{5,4},{6,7},{7,6},{8,9},{9,8},{10,11... | collective-permute-start | bytes 1572872 | tf_op jit(solution)/shard_map/while/body/eval_jaxpr/ppermute | solution.py:41
  400.5 6.6 %collective-permute-done.6.refs_1_ = bf16[160,1024]{1,0:T(8,128)(2,1)S(1)} collective-permute-done((bf16[160,1024]{1,0:T(8,128)(2,1)S(1)}, bf16[160,1024]{1,0:T(8,128)(2,1)S(1)}, u32[]{:S(2)}, u32[]{:S(2)}) %collective-permute-start.6) | collective-permute-done | bytes 327712 | tf_op jit(solution)/shard_map/while/body/eval_jaxpr/ppermute | solution.py:36
  424.1 6.7 %collective-permute-start.11 = (bf16[40,1024]{1,0:T(8,128)(2,1)S(1)}, bf16[40,1024]{1,0:T(8,128)(2,1)S(1)}, u32[]{:S(2)}, u32[]{:S(2)}) collective-permute-start(bf16[40,1024]{1,0:T(8,128)(2,1)S(1)} %get-tuple-element.586), channel_id=1, source_target_pairs={{0,6},{1,7},{2,0},{3,1},{4,2},{5,3},{6,4},{7,5},{8,14},{9,15},{10,... | collective-permute-start | bytes 245768 | tf_op jit(solution)/shard_map/while/body/eval_jaxpr/ppermute | solution.py:36
  433.2 5.6 collective-permute-done.12.refs_2_
  440.7 7.8 %collective-permute-start.14 = (f32[128,1024]{1,0:T(8,128)S(1)}, f32[128,1024]{1,0:T(8,128)S(1)}, u32[]{:S(2)}, u32[]{:S(2)}) collective-permute-start(f32[128,1024]{1,0:T(8,128)S(1)} %combine.10), channel_id=1, source_target_pairs={{0,1},{1,0},{2,3},{3,2},{4,5},{5,4},{6,7},{7,6},{8,9},{9,8},{10,11... | collective-permute-start | bytes 1572872 | tf_op jit(solution)/shard_map/while/body/eval_jaxpr/ppermute | solution.py:41
  468.6 7.9 %collective-permute-done.6.refs_1_ = bf16[160,1024]{1,0:T(8,128)(2,1)S(1)} collective-permute-done((bf16[160,1024]{1,0:T(8,128)(2,1)S(1)}, bf16[160,1024]{1,0:T(8,128)(2,1)S(1)}, u32[]{:S(2)}, u32[]{:S(2)}) %collective-permute-start.6) | collective-permute-done | bytes 327712 | tf_op jit(solution)/shard_map/while/body/eval_jaxpr/ppermute | solution.py:36
  507.3 7.8 %collective-permute-start.14 = (f32[128,1024]{1,0:T(8,128)S(1)}, f32[128,1024]{1,0:T(8,128)S(1)}, u32[]{:S(2)}, u32[]{:S(2)}) collective-permute-start(f32[128,1024]{1,0:T(8,128)S(1)} %combine.10), channel_id=1, source_target_pairs={{0,1},{1,0},{2,3},{3,2},{4,5},{5,4},{6,7},{7,6},{8,9},{9,8},{10,11... | collective-permute-start | bytes 1572872 | tf_op jit(solution)/shard_map/while/body/eval_jaxpr/ppermute | solution.py:41
  535.0 7.7 %collective-permute-done.6.refs_1_ = bf16[160,1024]{1,0:T(8,128)(2,1)S(1)} collective-permute-done((bf16[160,1024]{1,0:T(8,128)(2,1)S(1)}, bf16[160,1024]{1,0:T(8,128)(2,1)S(1)}, u32[]{:S(2)}, u32[]{:S(2)}) %collective-permute-start.6) | collective-permute-done | bytes 327712 | tf_op jit(solution)/shard_map/while/body/eval_jaxpr/ppermute | solution.py:36
  572.0 8.9 %collective-permute-start.14 = (f32[128,1024]{1,0:T(8,128)S(1)}, f32[128,1024]{1,0:T(8,128)S(1)}, u32[]{:S(2)}, u32[]{:S(2)}) collective-permute-start(f32[128,1024]{1,0:T(8,128)S(1)} %combine.10), channel_id=1, source_target_pairs={{0,1},{1,0},{2,3},{3,2},{4,5},{5,4},{6,7},{7,6},{8,9},{9,8},{10,11... | collective-permute-start | bytes 1572872 | tf_op jit(solution)/shard_map/while/body/eval_jaxpr/ppermute | solution.py:41
  601.2 7.9 %collective-permute-done.6.refs_1_ = bf16[160,1024]{1,0:T(8,128)(2,1)S(1)} collective-permute-done((bf16[160,1024]{1,0:T(8,128)(2,1)S(1)}, bf16[160,1024]{1,0:T(8,128)(2,1)S(1)}, u32[]{:S(2)}, u32[]{:S(2)}) %collective-permute-start.6) | collective-permute-done | bytes 327712 | tf_op jit(solution)/shard_map/while/body/eval_jaxpr/ppermute | solution.py:36
  638.5 8.9 %collective-permute-start.14 = (f32[128,1024]{1,0:T(8,128)S(1)}, f32[128,1024]{1,0:T(8,128)S(1)}, u32[]{:S(2)}, u32[]{:S(2)}) collective-permute-start(f32[128,1024]{1,0:T(8,128)S(1)} %combine.10), channel_id=1, source_target_pairs={{0,1},{1,0},{2,3},{3,2},{4,5},{5,4},{6,7},{7,6},{8,9},{9,8},{10,11... | collective-permute-start | bytes 1572872 | tf_op jit(solution)/shard_map/while/body/eval_jaxpr/ppermute | solution.py:41
  (481 shorter events, 456.5 us)
Async XLA Ops:
  31.5 54.8 %collective-permute-start.28 = (bf16[384,1024]{1,0:T(8,128)(2,1)}, bf16[384,1024]{1,0:T(8,128)(2,1)}, u32[]{:S(2)}, u32[]{:S(2)}) collective-permute-start(bf16[384,1024]{1,0:T(8,128)(2,1)} %get-tuple-element.449), channel_id=1, source_target_pairs={{0,8},{8,16},{16,24},{24,0},{1,9},{9,17},{17,25},{25,1},{2,10},{10... | collective-permute-start | bytes 2359304 | tf_op jit(solution)/shard_map/ppermute | solution.py:36
  32.8 57.6 %collective-permute-start.25 = (bf16[384,1024]{1,0:T(8,128)(2,1)S(1)}, bf16[384,1024]{1,0:T(8,128)(2,1)}, u32[]{:S(2)}, u32[]{:S(2)}) collective-permute-start(bf16[384,1024]{1,0:T(8,128)(2,1)S(1)} %get-tuple-element.451), channel_id=1, source_target_pairs={{0,24},{8,0},{16,8},{24,16},{1,25},{9,1},{17,9},{25,17},{2,26},{10... | collective-permute-start | bytes 2359304 | tf_op jit(solution)/shard_map/ppermute | solution.py:36
  34.2 56.3 %collective-permute-start.26 = (bf16[384,1024]{1,0:T(8,128)(2,1)S(1)}, bf16[384,1024]{1,0:T(8,128)(2,1)}, u32[]{:S(2)}, u32[]{:S(2)}) collective-permute-start(bf16[384,1024]{1,0:T(8,128)(2,1)S(1)} %get-tuple-element.450), channel_id=1, source_target_pairs={{0,16},{8,24},{16,0},{24,8},{1,17},{9,25},{17,1},{25,9},{2,18},{10... | collective-permute-start | bytes 2359304 | tf_op jit(solution)/shard_map/ppermute | solution.py:36
  35.6 39.2 %collective-permute-start.20 = (bf16[160,1024]{1,0:T(8,128)(2,1)S(1)}, bf16[160,1024]{1,0:T(8,128)(2,1)S(1)}, u32[]{:S(2)}, u32[]{:S(2)}) collective-permute-start(bf16[160,1024]{1,0:T(8,128)(2,1)S(1)} %constant_dynamic-update-slice_fusion.4.refs_0_), channel_id=1, source_target_pairs={{0,24},{8,0},{16,8},{24,16},{1,25},{9,1},{17,9},{25,17},{2,26},{10... | collective-permute-start | bytes 983048 | tf_op jit(solution)/shard_map/ppermute | solution.py:36
  36.8 41.9 %collective-permute-start.21 = (bf16[160,1024]{1,0:T(8,128)(2,1)S(1)}, bf16[160,1024]{1,0:T(8,128)(2,1)S(1)}, u32[]{:S(2)}, u32[]{:S(2)}) collective-permute-start(bf16[160,1024]{1,0:T(8,128)(2,1)S(1)} %constant_dynamic-update-slice_fusion.4.refs_0_), channel_id=1, source_target_pairs={{0,16},{8,24},{16,0},{24,8},{1,17},{9,25},{17,1},{25,9},{2,18},{10... | collective-permute-start | bytes 983048 | tf_op jit(solution)/shard_map/ppermute | solution.py:36
  134.7 12.4 %collective-permute-start.5 = (bf16[160,1024]{1,0:T(8,128)(2,1)S(1)}, bf16[160,1024]{1,0:T(8,128)(2,1)S(1)}, u32[]{:S(2)}, u32[]{:S(2)}) collective-permute-start(bf16[160,1024]{1,0:T(8,128)(2,1)S(1)} %constant_dynamic-update-slice_fusion.15.refs_0_), channel_id=1, source_target_pairs={{0,16},{8,24},{16,0},{24,8},{1,17},{9,25},{17,1},{25,9},{2,18},{10... | collective-permute-start | bytes 983048 | tf_op jit(solution)/shard_map/while/body/eval_jaxpr/ppermute | solution.py:36
  134.9 14.0 %collective-permute-start.7 = (bf16[128,1024]{1,0:T(8,128)(2,1)S(1)}, bf16[128,1024]{1,0:T(8,128)(2,1)S(1)}, u32[]{:S(2)}, u32[]{:S(2)}) collective-permute-start(bf16[128,1024]{1,0:T(8,128)(2,1)S(1)} %copy-done.6), channel_id=1, source_target_pairs={{0,32},{32,64},{64,96},{96,128},{128,160},{160,192},{192,224},{224... | collective-permute-start | bytes 786440 | tf_op jit(solution)/shard_map/while/body/eval_jaxpr/ppermute | solution.py:36
  184.8 12.8 %collective-permute-start.2 = (bf16[40,1024]{1,0:T(8,128)(2,1)S(1)}, bf16[40,1024]{1,0:T(8,128)(2,1)S(1)}, u32[]{:S(2)}, u32[]{:S(2)}) collective-permute-start(bf16[40,1024]{1,0:T(8,128)(2,1)S(1)} %get-tuple-element.579), channel_id=1, source_target_pairs={{0,36},{1,37},{2,38},{3,39},{4,32},{5,33},{6,34},{7,35},{32,68},{3... | collective-permute-start | bytes 245768 | tf_op jit(solution)/shard_map/while/body/eval_jaxpr/ppermute | solution.py:51
  197.8 13.2 %collective-permute-start.4 = (bf16[160,1024]{1,0:T(8,128)(2,1)S(1)}, bf16[160,1024]{1,0:T(8,128)(2,1)S(1)}, u32[]{:S(2)}, u32[]{:S(2)}) collective-permute-start(bf16[160,1024]{1,0:T(8,128)(2,1)S(1)} %constant_dynamic-update-slice_fusion.15.refs_0_), channel_id=1, source_target_pairs={{0,24},{8,0},{16,8},{24,16},{1,25},{9,1},{17,9},{25,17},{2,26},{10... | collective-permute-start | bytes 983048 | tf_op jit(solution)/shard_map/while/body/eval_jaxpr/ppermute | solution.py:36
  200.4 12.4 %collective-permute-start.5 = (bf16[160,1024]{1,0:T(8,128)(2,1)S(1)}, bf16[160,1024]{1,0:T(8,128)(2,1)S(1)}, u32[]{:S(2)}, u32[]{:S(2)}) collective-permute-start(bf16[160,1024]{1,0:T(8,128)(2,1)S(1)} %constant_dynamic-update-slice_fusion.15.refs_0_), channel_id=1, source_target_pairs={{0,16},{8,24},{16,0},{24,8},{1,17},{9,25},{17,1},{25,9},{2,18},{10... | collective-permute-start | bytes 983048 | tf_op jit(solution)/shard_map/while/body/eval_jaxpr/ppermute | solution.py:36
  200.4 14.2 %collective-permute-start.7 = (bf16[128,1024]{1,0:T(8,128)(2,1)S(1)}, bf16[128,1024]{1,0:T(8,128)(2,1)S(1)}, u32[]{:S(2)}, u32[]{:S(2)}) collective-permute-start(bf16[128,1024]{1,0:T(8,128)(2,1)S(1)} %copy-done.6), channel_id=1, source_target_pairs={{0,32},{32,64},{64,96},{96,128},{128,160},{160,192},{192,224},{224... | collective-permute-start | bytes 786440 | tf_op jit(solution)/shard_map/while/body/eval_jaxpr/ppermute | solution.py:36
  266.6 12.7 %collective-permute-start.5 = (bf16[160,1024]{1,0:T(8,128)(2,1)S(1)}, bf16[160,1024]{1,0:T(8,128)(2,1)S(1)}, u32[]{:S(2)}, u32[]{:S(2)}) collective-permute-start(bf16[160,1024]{1,0:T(8,128)(2,1)S(1)} %constant_dynamic-update-slice_fusion.15.refs_0_), channel_id=1, source_target_pairs={{0,16},{8,24},{16,0},{24,8},{1,17},{9,25},{17,1},{25,9},{2,18},{10... | collective-permute-start | bytes 983048 | tf_op jit(solution)/shard_map/while/body/eval_jaxpr/ppermute | solution.py:36
  266.6 14.5 %collective-permute-start.7 = (bf16[128,1024]{1,0:T(8,128)(2,1)S(1)}, bf16[128,1024]{1,0:T(8,128)(2,1)S(1)}, u32[]{:S(2)}, u32[]{:S(2)}) collective-permute-start(bf16[128,1024]{1,0:T(8,128)(2,1)S(1)} %copy-done.6), channel_id=1, source_target_pairs={{0,32},{32,64},{64,96},{96,128},{128,160},{160,192},{192,224},{224... | collective-permute-start | bytes 786440 | tf_op jit(solution)/shard_map/while/body/eval_jaxpr/ppermute | solution.py:36
  333.1 13.8 %collective-permute-start.7 = (bf16[128,1024]{1,0:T(8,128)(2,1)S(1)}, bf16[128,1024]{1,0:T(8,128)(2,1)S(1)}, u32[]{:S(2)}, u32[]{:S(2)}) collective-permute-start(bf16[128,1024]{1,0:T(8,128)(2,1)S(1)} %copy-done.6), channel_id=1, source_target_pairs={{0,32},{32,64},{64,96},{96,128},{128,160},{160,192},{192,224},{224... | collective-permute-start | bytes 786440 | tf_op jit(solution)/shard_map/while/body/eval_jaxpr/ppermute | solution.py:36
  400.5 13.9 %collective-permute-start.7 = (bf16[128,1024]{1,0:T(8,128)(2,1)S(1)}, bf16[128,1024]{1,0:T(8,128)(2,1)S(1)}, u32[]{:S(2)}, u32[]{:S(2)}) collective-permute-start(bf16[128,1024]{1,0:T(8,128)(2,1)S(1)} %copy-done.6), channel_id=1, source_target_pairs={{0,32},{32,64},{64,96},{96,128},{128,160},{160,192},{192,224},{224... | collective-permute-start | bytes 786440 | tf_op jit(solution)/shard_map/while/body/eval_jaxpr/ppermute | solution.py:36
  465.9 13.2 %collective-permute-start.4 = (bf16[160,1024]{1,0:T(8,128)(2,1)S(1)}, bf16[160,1024]{1,0:T(8,128)(2,1)S(1)}, u32[]{:S(2)}, u32[]{:S(2)}) collective-permute-start(bf16[160,1024]{1,0:T(8,128)(2,1)S(1)} %constant_dynamic-update-slice_fusion.15.refs_0_), channel_id=1, source_target_pairs={{0,24},{8,0},{16,8},{24,16},{1,25},{9,1},{17,9},{25,17},{2,26},{10... | collective-permute-start | bytes 983048 | tf_op jit(solution)/shard_map/while/body/eval_jaxpr/ppermute | solution.py:36
  468.6 13.5 %collective-permute-start.5 = (bf16[160,1024]{1,0:T(8,128)(2,1)S(1)}, bf16[160,1024]{1,0:T(8,128)(2,1)S(1)}, u32[]{:S(2)}, u32[]{:S(2)}) collective-permute-start(bf16[160,1024]{1,0:T(8,128)(2,1)S(1)} %constant_dynamic-update-slice_fusion.15.refs_0_), channel_id=1, source_target_pairs={{0,16},{8,24},{16,0},{24,8},{1,17},{9,25},{17,1},{25,9},{2,18},{10... | collective-permute-start | bytes 983048 | tf_op jit(solution)/shard_map/while/body/eval_jaxpr/ppermute | solution.py:36
  468.6 15.2 %collective-permute-start.7 = (bf16[128,1024]{1,0:T(8,128)(2,1)S(1)}, bf16[128,1024]{1,0:T(8,128)(2,1)S(1)}, u32[]{:S(2)}, u32[]{:S(2)}) collective-permute-start(bf16[128,1024]{1,0:T(8,128)(2,1)S(1)} %copy-done.6), channel_id=1, source_target_pairs={{0,32},{32,64},{64,96},{96,128},{128,160},{160,192},{192,224},{224... | collective-permute-start | bytes 786440 | tf_op jit(solution)/shard_map/while/body/eval_jaxpr/ppermute | solution.py:36
  532.3 13.1 %collective-permute-start.4 = (bf16[160,1024]{1,0:T(8,128)(2,1)S(1)}, bf16[160,1024]{1,0:T(8,128)(2,1)S(1)}, u32[]{:S(2)}, u32[]{:S(2)}) collective-permute-start(bf16[160,1024]{1,0:T(8,128)(2,1)S(1)} %constant_dynamic-update-slice_fusion.15.refs_0_), channel_id=1, source_target_pairs={{0,24},{8,0},{16,8},{24,16},{1,25},{9,1},{17,9},{25,17},{2,26},{10... | collective-permute-start | bytes 983048 | tf_op jit(solution)/shard_map/while/body/eval_jaxpr/ppermute | solution.py:36
  535.0 13.2 %collective-permute-start.5 = (bf16[160,1024]{1,0:T(8,128)(2,1)S(1)}, bf16[160,1024]{1,0:T(8,128)(2,1)S(1)}, u32[]{:S(2)}, u32[]{:S(2)}) collective-permute-start(bf16[160,1024]{1,0:T(8,128)(2,1)S(1)} %constant_dynamic-update-slice_fusion.15.refs_0_), channel_id=1, source_target_pairs={{0,16},{8,24},{16,0},{24,8},{1,17},{9,25},{17,1},{25,9},{2,18},{10... | collective-permute-start | bytes 983048 | tf_op jit(solution)/shard_map/while/body/eval_jaxpr/ppermute | solution.py:36
  535.0 15.0 %collective-permute-start.7 = (bf16[128,1024]{1,0:T(8,128)(2,1)S(1)}, bf16[128,1024]{1,0:T(8,128)(2,1)S(1)}, u32[]{:S(2)}, u32[]{:S(2)}) collective-permute-start(bf16[128,1024]{1,0:T(8,128)(2,1)S(1)} %copy-done.6), channel_id=1, source_target_pairs={{0,32},{32,64},{64,96},{96,128},{128,160},{160,192},{192,224},{224... | collective-permute-start | bytes 786440 | tf_op jit(solution)/shard_map/while/body/eval_jaxpr/ppermute | solution.py:36
  598.5 13.2 %collective-permute-start.4 = (bf16[160,1024]{1,0:T(8,128)(2,1)S(1)}, bf16[160,1024]{1,0:T(8,128)(2,1)S(1)}, u32[]{:S(2)}, u32[]{:S(2)}) collective-permute-start(bf16[160,1024]{1,0:T(8,128)(2,1)S(1)} %constant_dynamic-update-slice_fusion.15.refs_0_), channel_id=1, source_target_pairs={{0,24},{8,0},{16,8},{24,16},{1,25},{9,1},{17,9},{25,17},{2,26},{10... | collective-permute-start | bytes 983048 | tf_op jit(solution)/shard_map/while/body/eval_jaxpr/ppermute | solution.py:36
  601.2 13.5 %collective-permute-start.5 = (bf16[160,1024]{1,0:T(8,128)(2,1)S(1)}, bf16[160,1024]{1,0:T(8,128)(2,1)S(1)}, u32[]{:S(2)}, u32[]{:S(2)}) collective-permute-start(bf16[160,1024]{1,0:T(8,128)(2,1)S(1)} %constant_dynamic-update-slice_fusion.15.refs_0_), channel_id=1, source_target_pairs={{0,16},{8,24},{16,0},{24,8},{1,17},{9,25},{17,1},{25,9},{2,18},{10... | collective-permute-start | bytes 983048 | tf_op jit(solution)/shard_map/while/body/eval_jaxpr/ppermute | solution.py:36
  601.2 15.3 %collective-permute-start.7 = (bf16[128,1024]{1,0:T(8,128)(2,1)S(1)}, bf16[128,1024]{1,0:T(8,128)(2,1)S(1)}, u32[]{:S(2)}, u32[]{:S(2)}) collective-permute-start(bf16[128,1024]{1,0:T(8,128)(2,1)S(1)} %copy-done.6), channel_id=1, source_target_pairs={{0,32},{32,64},{64,96},{96,128},{128,160},{160,192},{192,224},{224... | collective-permute-start | bytes 786440 | tf_op jit(solution)/shard_map/while/body/eval_jaxpr/ppermute | solution.py:36
  (166 other events, 1652.1 us)
where the time goes:
time: 652 us; the launch traced here: 651 us
  starting transfers between devices  272 us (42%)
  waiting for transfers between devices  260 us (40%)
  Pallas kernels  99 us (15%)
  local copies, waits for them, and re-layouts  13.3 us (2%)
    ppermute x96, waiting for transfers between devices, shifted(): lax.ppermute(block, axis, [(i, (i + distance) % size) for i in range(size)])  201 us
    ppermute x96, starting transfers between devices, shifted(): lax.ppermute(block, axis, [(i, (i + distance) % size) for i in range(size)])  142 us
    ppermute x11, starting transfers between devices, core_swap(): return lax.ppermute(block, 'expert', [(i, i ^ 1) for i in range(size)])  71.8 us
    ppermute x32, starting transfers between devices, onward(): return lax.ppermute(block, ('pipe', 'expert'), route)  58.6 us
    ppermute x32, waiting for transfers between devices, onward(): return lax.ppermute(block, ('pipe', 'expert'), route)  45.8 us
    pallas_call x9, Pallas kernels, expert_work(): partial = gate_up[0](*weights, *(slices[k] for k in early))  23.9 us
    pallas_call x9, Pallas kernels, expert_work(): down[0](*(hiddens[k] for k in early), *(down_parts[k] for k in early))  17 us
    pallas_call x9, Pallas kernels, expert_work(): hidden = gate_up[1](*weights, *(slices[k] for k in late), *partial)  15.8 us
  transfers between devices with their start and end apart: 139, of which 89 were waited for; matrix products, arithmetic and copies ran while one was open for 1% of the time, Pallas kernels for 9%

commit v1 on v0

--- a/solution.py
+++ b/solution.py
@@ -18,10 +18,9 @@
 RANK_SHIFTS = (2, 1, 3)
 
 
-def kernel_call(body, name, in_specs, out_shapes, mib, scratch=(), flops=0, moved=0):
+def kernel_call(body, in_specs, out_shapes, mib, scratch=(), flops=0, moved=0):
     return pl.pallas_call(
         body,
-        name=name,
         in_specs=in_specs,
         out_specs=jax.tree.map(lambda _: VMEM, out_shapes),
         out_shape=out_shapes,
@@ -29,6 +28,10 @@
         compiler_params=pltpu.CompilerParams(vmem_limit_bytes=mib << 20),
         cost_estimate=pl.CostEstimate(flops=flops, bytes_accessed=moved, transcendentals=0),
     )
+
+
+def in_hbm(value):
+    return pltpu.with_memory_space_constraint(value, pltpu.HBM)
 
 
 def shifted(block, axis, distance):
@@ -112,67 +115,68 @@
     out[...] = update + jnp.dot(low[which[0]], rows, preferred_element_type=f32)
 
 
-def gate_up_kernel(shifts, last, model_width, rank, gains, w_gate, w_up, *refs):
-    count = len(shifts)
-    slices = refs[:count]
-    refs = refs[count:]
-    if last:
-        gate_in, up_in, squares_in, hidden, gate_buf, up_buf, sems = refs
-    else:
-        gate_out, up_out, squares_out, gate_buf, up_buf, sems = refs
+def gate_up_first(early, late, rank, gains, w_gate, w_up, *refs):
+    count, downs = len(early), len(early) + len(late)
+    w_down, refs = refs[:downs], refs[downs:]
+    slices, refs = refs[:count], refs[count:]
+    gate_out, up_out, squares_out, gate_late, up_late, down_out, gate_buf, up_buf, sems, late_sems, down_sems = refs
     width = slices[0].shape[1]
     ranks = w_gate.shape[0] // width
-    copies = []
-    for i, k in enumerate(shifts):
+
+    def pair(k, i, gate_to, up_to, sems):
         start = lax.rem(rank[0] + (ranks - k), ranks) * width
-        pair = [
-            pltpu.make_async_copy(src.at[pl.ds(start, width)], buf.at[i], sems.at[i, j])
-            for j, (src, buf) in enumerate(((w_gate, gate_buf), (w_up, up_buf)))
+        return [
+            pltpu.make_async_copy(w_gate.at[pl.ds(start, width)], gate_to.at[i], sems.at[i, 0]),
+            pltpu.make_async_copy(w_up.at[pl.ds(start, width)], up_to.at[i], sems.at[i, 1]),
         ]
-        for copy in pair:
-            copy.start()
-        copies.append(pair)
-    if last:
-        gate, up, squares = gate_in[...], up_in[...], squares_in[:, :1]
-    else:
-        gate, up, squares = 0.0, 0.0, 0.0
-    for i, k in enumerate(shifts):
+
+    now = [pair(k, i, gate_buf, up_buf, sems) for i, k in enumerate(early)]
+    later = [copy for i, k in enumerate(late) for copy in pair(k, i, gate_late, up_late, late_sems)]
+    later += [pltpu.make_async_copy(w_down[i], down_out.at[i], down_sems.at[i]) for i in range(downs)]
+    for copy in [*now[0], *now[1], *later]:
+        copy.start()
+    gate, up, squares = 0.0, 0.0, 0.0
+    for i, k in enumerate(early):
         wide = slices[i][...].astype(f32)
         squares = squares + jnp.sum(wide * wide, axis=1, keepdims=True)
         scaled = (wide * gains[k : k + 1]).astype(bf16)
-        copies[i][0].wait()
+        now[i][0].wait()
         gate = gate + jnp.dot(scaled, gate_buf[i], preferred_element_type=f32)
-        copies[i][1].wait()
+        now[i][1].wait()
         up = up + jnp.dot(scaled, up_buf[i], preferred_element_type=f32)
-    if last:
-        inv_rms = lax.rsqrt(squares * (1.0 / model_width) + epsilon)
-        gate = gate * inv_rms
-        hidden[...] = (gate / (1.0 + jnp.exp(-gate)) * (up * inv_rms)).astype(bf16)
-    else:
-        gate_out[...] = gate
-        up_out[...] = up
-        squares_out[...] = jnp.broadcast_to(squares, squares_out.shape)
-
-
-def down_kernel(last, count, *refs):
-    parts, matrices, refs = refs[:count], refs[count : 2 * count], refs[2 * count :]
-    if last:
-        before, *outs, buf, sems = refs
-    else:
-        out, buf, sems = refs
-    copies = [pltpu.make_async_copy(matrices[i], buf.at[i], sems.at[i]) for i in range(count)]
-    for copy in copies:
-        copy.start()
-    total = before[...] if last else 0.0
-    for i in range(count):
-        copies[i].wait()
-        total = total + jnp.dot(parts[i][...], buf[i], preferred_element_type=f32)
-    if last:
-        size = outs[0].shape[0]
-        for k, piece in enumerate(outs):
-            piece[...] = total[k * size : (k + 1) * size].astype(bf16)
-    else:
-        out[...] = total
+    gate_out[...] = gate
+    up_out[...] = up
+    squares_out[...] = jnp.broadcast_to(squares, squares_out.shape)
+    for copy in later:
+        copy.wait()
+
+
+def gate_up_last(late, model_width, gains, gate_late, up_late, gate_in, up_in, squares_in, *refs):
+    *slices, hidden = refs
+    gate, up, squares = gate_in[...], up_in[...], squares_in[:, :1]
+    for i, k in enumerate(late):
+        wide = slices[i][...].astype(f32)
+        squares = squares + jnp.sum(wide * wide, axis=1, keepdims=True)
+        scaled = (wide * gains[k : k + 1]).astype(bf16)
+        gate = gate + jnp.dot(scaled, gate_late[i], preferred_element_type=f32)
+        up = up + jnp.dot(scaled, up_late[i], preferred_element_type=f32)
+    inv_rms = lax.rsqrt(squares * (1.0 / model_width) + epsilon)
+    gate = gate * inv_rms
+    hidden[...] = (gate / (1.0 + jnp.exp(-gate)) * (up * inv_rms)).astype(bf16)
+
+
+def down_first(matrices, own, guest, out):
+    out[...] = jnp.dot(own[...], matrices[0], preferred_element_type=f32) + jnp.dot(
+        guest[...], matrices[1], preferred_element_type=f32
+    )
+
+
+def down_last(matrices, before, one, other, *outs):
+    total = before[...] + jnp.dot(one[...], matrices[2], preferred_element_type=f32)
+    total = total + jnp.dot(other[...], matrices[3], preferred_element_type=f32)
+    size = outs[0].shape[0]
+    for k, piece in enumerate(outs):
+        piece[...] = total[k * size : (k + 1) * size].astype(bf16)
 
 
 def local(tokens, gains, route_ids, route_weights, picks, w_gate, w_up, w_down):
@@ -203,7 +207,10 @@
         return jnp.concatenate([first, second], axis=dim)
 
     def shape(*dims, kind=bf16):
-        return jax.ShapeDtypeStruct(dims, kind)
+        return pltpu.VMEM(dims, kind)
+
+    down_parts = {k: shifted(slice_at(down_matrix, rank + k, 1), "tensor", k) for k in RANK_SHIFTS}
+    down_parts[0] = slice_at(down_matrix, rank, 1)
 
     info = jnp.concatenate(
         [route_ids[0].transpose(0, 2, 1).astype(f32), picks[0].astype(f32), route_weights[0].transpose(0, 2, 1)],
@@ -213,56 +220,35 @@
     where = jnp.stack([chip, core]).astype(i32)
     table = shape(micro_count, 2 * local_tokens, rows)
     tables = kernel_call(
-        functools.partial(tables_kernel, (chips, ranks, quarter, capacity)),
-        "tables",
-        (SMEM, VMEM),
-        (table, table, table),
-        8,
+        functools.partial(tables_kernel, (chips, ranks, quarter, capacity)), (SMEM, VMEM), (table, table, table), 8
     )
     first_place, high, low = tables(where, info)
 
     own_slice = lax.dynamic_slice_in_dim(tokens, rank * width, width, 2)
     entering = by_core(own_slice, core_swap(own_slice), 1)
 
-    dispatch = kernel_call(
-        dispatch_kernel, "dispatch", (SMEM, VMEM, VMEM), (shape(per_chip, width),) * chips, 8, flops=10**9
-    )
+    dispatch = kernel_call(dispatch_kernel, (SMEM, VMEM, VMEM), (shape(per_chip, width),) * chips, 8, flops=10**9)
     combine = kernel_call(
-        combine_kernel,
-        "combine",
-        (SMEM, VMEM, VMEM) + (VMEM,) * chips,
-        shape(2 * local_tokens, width, kind=f32),
-        8,
-        flops=10**9,
-    )
-    half = (shape(rows, hidden_width, kind=f32),) * 2 + (shape(rows, 128, kind=f32),)
-    buffers = [pltpu.VMEM((2, width, hidden_width), bf16)] * 2 + [pltpu.SemaphoreType.DMA((2, 2))]
+        combine_kernel, (SMEM, VMEM, VMEM) + (VMEM,) * chips, shape(2 * local_tokens, width, kind=f32), 8, flops=10**9
+    )
     early, late = (0, 1), (3, 2)
-    gate_up = [
-        kernel_call(
-            functools.partial(gate_up_kernel, shifts, last, model_width),
-            name,
-            (SMEM, VMEM, HBM, HBM, VMEM, VMEM) + (VMEM,) * (3 * last),
-            shape(rows, hidden_width) if last else half,
-            16,
-            buffers,
-            flops=2 * 10**9,
-        )
-        for name, shifts, last in (("gate_up_a", early, False), ("gate_up_b", late, True))
-    ]
-    down_buffers = [pltpu.VMEM((2, hidden_width, width), bf16), pltpu.SemaphoreType.DMA((2,))]
-    down = [
-        kernel_call(
-            functools.partial(down_kernel, last, 2),
-            name,
-            (VMEM, VMEM, HBM, HBM) + (VMEM,) * last,
-            (shape(per_chip, width),) * chips if last else shape(rows, width, kind=f32),
-            10,
-            down_buffers,
-            flops=10**9,
-        )
-        for name, last in (("down_a", False), ("down_b", True))
-    ]
+    gate_up_a = kernel_call(
+        functools.partial(gate_up_first, early, late),
+        (SMEM, VMEM, HBM, HBM) + (HBM,) * ranks + (VMEM,) * 2,
+        (shape(rows, hidden_width, kind=f32),) * 2
+        + (shape(rows, 128, kind=f32),)
+        + (shape(2, width, hidden_width),) * 2
+        + (shape(ranks, hidden_width, width),),
+        24,
+        [pltpu.VMEM((2, width, hidden_width), bf16)] * 2
+        + [pltpu.SemaphoreType.DMA((2, 2)), pltpu.SemaphoreType.DMA((2, 2)), pltpu.SemaphoreType.DMA((ranks,))],
+        flops=3 * 10**9,
+    )
+    gate_up_b = kernel_call(
+        functools.partial(gate_up_last, late, model_width), (VMEM,) * 8, shape(rows, hidden_width), 16, flops=10**9
+    )
+    down_a = kernel_call(down_first, (VMEM,) * 3, shape(rows, width, kind=f32), 16, flops=5 * 10**8)
+    down_b = kernel_call(down_last, (VMEM,) * 4, (shape(per_chip, width),) * chips, 16, flops=5 * 10**8)
 
     rank_word = rank.reshape(1).astype(i32)
     gain_parts = jnp.concatenate([slice_at(gains, rank - k, 1) for k in range(ranks)])
@@ -271,14 +257,16 @@
         own = jnp.concatenate(blocks)
         slices = {k: shifted(own, "tensor", k) for k in RANK_SHIFTS}
         slices[0] = own
-        weights = (rank_word, gain_parts, gate_matrix, up_matrix)
-        partial = gate_up[0](*weights, *(slices[k] for k in early))
-        hidden = gate_up[1](*weights, *(slices[k] for k in late), *partial)
+        weights = [in_hbm(value) for value in (gate_matrix, up_matrix, *(down_parts[k] for k in (*early, *late)))]
+        gate, up, squares, gate_late, up_late, matrices = gate_up_a(
+            rank_word, gain_parts, *weights, *(slices[k] for k in early)
+        )
+        hidden = gate_up_b(gain_parts, gate_late, up_late, gate, up, squares, *(slices[k] for k in late))
         hidden, also = lax.optimization_barrier((hidden, also))
         hiddens = {k: shifted(hidden, "tensor", k) for k in RANK_SHIFTS}
         hiddens[0] = hidden
-        total = down[0](*(hiddens[k] for k in early), *(down_parts[k] for k in early))
-        return down[1](*(hiddens[k] for k in late), *(down_parts[k] for k in late), total), also
+        total = down_a(matrices, *(hiddens[k] for k in early))
+        return down_b(matrices, total, *(hiddens[k] for k in late)), also
 
     def to_home(blocks):
         back = {k: shifted(blocks[k], "expert", groups - 2 * k) for k in CHIP_SHIFTS}
@@ -290,21 +278,21 @@
         return (stream.astype(f32) + (update + core_swap(update))).astype(bf16)
 
     def kept(collected, fresh, spot):
-        own = lax.dynamic_slice_in_dim(fresh, core * local_tokens, local_tokens)
-        return lax.dynamic_update_slice_in_dim(collected, own[None], spot, 0)
+        own = lax.dynamic_slice_in_dim(fresh, core * local_tokens, local_tokens)[None]
+        held = lax.dynamic_slice_in_dim(collected, jnp.minimum(spot, micro_count - 1), 1)
+        own = jnp.where(spot < micro_count, own, held)
+        return lax.dynamic_update_slice_in_dim(collected, own, jnp.minimum(spot, micro_count - 1), 0)
 
     outgoing = dispatch(jnp.zeros(1, i32), first_place, entering[0])
     moved = {k: shifted(outgoing[k], "expert", 2 * k) for k in CHIP_SHIFTS}
     moved[0] = outgoing[0]
 
-    down_parts = {k: shifted(slice_at(down_matrix, rank + k, 1), "tensor", k) for k in RANK_SHIFTS}
-    down_parts[0] = slice_at(down_matrix, rank, 1)
     next_info = shifted(info, "pipe", sections - 1)
     place = tables(where, next_info)[0]
 
     blocks, stream = expert_work([moved[k] for k in range(chips)], down_parts, entering[0])
     fresh = combined(stream, to_home(blocks), jnp.zeros((), i32))
-    collected = kept(jnp.zeros((micro_count + 1, local_tokens, width), bf16), fresh, 0)
+    collected = kept(jnp.zeros((micro_count, local_tokens, width), bf16), fresh, 0)
     fresh = jnp.where(section == sections - 1, entering[1], fresh)
 
     def tick(index, carry):
@@ -319,7 +307,7 @@
         return fresh, kept(collected, fresh, jnp.clip(unit, 0, micro_count))
 
     fresh, collected = lax.fori_loop(1, micro_count + sections - 1, tick, (fresh, collected))
-    return collected[None, :micro_count]
+    return collected[None]
 
 
 def solution(mesh):

time: 652 us -> 580 us (0.89)
  Pallas kernels: 99 us -> 60.5 us
  starting transfers between devices: 272 us -> 253 us
  local copies, waits for them, and re-layouts: 13.3 us -> 5.34 us
    ppermute x11, starting transfers between devices: 71.8 us -> 40.3 us  [core_swap(): return lax.ppermute(block, 'expert', [(i, i ^ 1) for i in range(size)])]
    pallas_call x36, Pallas kernels: 72.2 us -> 52.5 us  [the longest x9 35.2 us: expert_work(): gate_up_a(rank_word, gain_parts, *weights, *(slices[k] for k in early))]
    ppermute x96, starting transfers between devices: 142 us -> 161 us  [shifted(): lax.ppermute(block, axis, [(i, (i + distance) % size) for i in range(size)])]
    pallas_call x8, Pallas kernels: 11.5 us -> 2.12 us  [tick(): outgoing = dispatch(leaving.reshape(1), place, fresh)]
    pallas_call x9, Pallas kernels: 11.2 us -> 2.55 us  [combined(): update = combine(which.reshape(1), high, low, *blocks)]
    ppermute x96, waiting for transfers between devices: 201 us -> 192 us  [shifted(): lax.ppermute(block, axis, [(i, (i + distance) % size) for i in range(size)])]
    ppermute x32, starting transfers between devices: 58.6 us -> 51.8 us  [onward(): return lax.ppermute(block, ('pipe', 'expert'), route)]
  transfers between devices with their start and end apart: 139 -> 139, of which waited for: 89 -> 90; matrix products, arithmetic and copies ran while one was open for 1% -> 1% of each run, Pallas kernels for 9% -> 9%
where the time goes in v1:
time: 580 us
  waiting for transfers between devices  255 us (44%)
  starting transfers between devices  253 us (44%)
  Pallas kernels  60.5 us (10%)
    ppermute x96, waiting for transfers between devices, shifted(): lax.ppermute(block, axis, [(i, (i + distance) % size) for i in range(size)])  192 us
    ppermute x96, starting transfers between devices, shifted(): lax.ppermute(block, axis, [(i, (i + distance) % size) for i in range(size)])  161 us
    ppermute x32, starting transfers between devices, onward(): return lax.ppermute(block, ('pipe', 'expert'), route)  51.8 us
    ppermute x32, waiting for transfers between devices, onward(): return lax.ppermute(block, ('pipe', 'expert'), route)  50.7 us
    ppermute x11, starting transfers between devices, core_swap(): return lax.ppermute(block, 'expert', [(i, i ^ 1) for i in range(size)])  40.3 us
    pallas_call x9, Pallas kernels, expert_work(): gate_up_a(rank_word, gain_parts, *weights, *(slices[k] for k in early))  35.2 us
    ppermute x11, waiting for transfers between devices, core_swap(): return lax.ppermute(block, 'expert', [(i, i ^ 1) for i in range(size)])  12.3 us
  transfers between devices with their start and end apart: 139, of which 90 were waited for; matrix products, arithmetic and copies ran while one was open for 1% of the time, Pallas kernels for 9%

profile of v1, /device:TPU:1, one launch (start us, length us, event | category | flops | bytes accessed | tf_op | source)
XLA Modules:
  0.0 580.3 jit_solution(15457199385522398914)
XLA Ops:
  18.2 5.1 collective-permute-start.21
  34.0 20.2 %collective-permute-done.23.refs_5_ = bf16[160,1024]{1,0:T(8,128)(2,1)S(1)} collective-permute-done((bf16[160,1024]{1,0:T(8,128)(2,1)S(1)}, bf16[160,1024]{1,0:T(8,128)(2,1)S(1)}, u32[]{:S(2)}, u32[]{:S(2)}) %collective-permute-start.23) | collective-permute-done | bytes 327712 | tf_op jit(solution)/shard_map/ppermute | solution.py:39
  58.8 5.4 collective-permute-done.25.refs_1_
  73.8 5.4 collective-permute-start.29
  98.9 480.7 %while.17 = (s32[]{:T(128)}, bf16[128,1024]{1,0:T(8,128)(2,1)S(1)}, bf16[2,64,1024]{2,1,0:T(8,128)(2,1)S(1)}, s32[]{:T(128)}, pred[]{:T(512)}, /*index=5*/bf16[2...) while((s32[]{:T(128)}, bf16[128,1024]{1,0:T(8,128)(2,1)S(1)}, ...), condition=%wide.region_1.2_spmd, body=%wide.region_0.1_spmd.sunk | while | flops 7000589824 | bytes 13468564 | solution.py:309
  135.4 8.1 %collective-permute-start.11 = (bf16[40,1024]{1,0:T(8,128)(2,1)S(1)}, bf16[40,1024]{1,0:T(8,128)(2,1)S(1)}, u32[]{:S(2)}, u32[]{:S(2)}) collective-permute-start(bf16[40,1024]{1,0:T(8,128)(2,1)S(1)} %get-tuple-element.601), channel_id=1, source_target_pairs={{0,6},{1,7},{2,0},{3,1},{4,2},{5,3},{6,4},{7,5},{8,14},{9,15},{10,... | collective-permute-start | bytes 245768 | tf_op jit(solution)/shard_map/while/body/eval_jaxpr/ppermute | solution.py:39
  146.0 5.1 collective-permute-done.12.refs_2_
  151.4 7.0 %collective-permute-start.14 = (f32[128,1024]{1,0:T(8,128)S(1)}, f32[128,1024]{1,0:T(8,128)S(1)}, u32[]{:S(2)}, u32[]{:S(2)}) collective-permute-start(f32[128,1024]{1,0:T(8,128)S(1)} %eval_jaxpr.46), channel_id=1, source_target_pairs={{0,1},{1,0},{2,3},{3,2},{4,5},{5,4},{6,7},{7,6},{8,9},{9,8},{10,11... | collective-permute-start | bytes 1572872 | tf_op jit(solution)/shard_map/while/body/eval_jaxpr/ppermute | solution.py:44
  258.4 5.1 collective-permute-start.11
  287.9 5.2 collective-permute-done.2
  318.8 6.0 %collective-permute-start.11 = (bf16[40,1024]{1,0:T(8,128)(2,1)S(1)}, bf16[40,1024]{1,0:T(8,128)(2,1)S(1)}, u32[]{:S(2)}, u32[]{:S(2)}) collective-permute-start(bf16[40,1024]{1,0:T(8,128)(2,1)S(1)} %get-tuple-element.601), channel_id=1, source_target_pairs={{0,6},{1,7},{2,0},{3,1},{4,2},{5,3},{6,4},{7,5},{8,14},{9,15},{10,... | collective-permute-start | bytes 245768 | tf_op jit(solution)/shard_map/while/body/eval_jaxpr/ppermute | solution.py:39
  328.3 5.6 collective-permute-done.12.refs_2_
  356.8 6.6 %collective-permute-done.4.refs_5_ = bf16[160,1024]{1,0:T(8,128)(2,1)S(1)} collective-permute-done((bf16[160,1024]{1,0:T(8,128)(2,1)S(1)}, bf16[160,1024]{1,0:T(8,128)(2,1)S(1)}, u32[]{:S(2)}, u32[]{:S(2)}) %collective-permute-start.4) | collective-permute-done | bytes 327712 | tf_op jit(solution)/shard_map/while/body/eval_jaxpr/ppermute | solution.py:39
  377.9 5.5 collective-permute-start.11
  386.7 5.1 collective-permute-done.12.refs_2_
  392.1 5.5 collective-permute-start.14
  406.9 5.7 collective-permute-done.2
  415.4 8.6 %collective-permute-done.4.refs_5_ = bf16[160,1024]{1,0:T(8,128)(2,1)S(1)} collective-permute-done((bf16[160,1024]{1,0:T(8,128)(2,1)S(1)}, bf16[160,1024]{1,0:T(8,128)(2,1)S(1)}, u32[]{:S(2)}, u32[]{:S(2)}) %collective-permute-start.4) | collective-permute-done | bytes 327712 | tf_op jit(solution)/shard_map/while/body/eval_jaxpr/ppermute | solution.py:39
  436.6 7.9 %collective-permute-start.11 = (bf16[40,1024]{1,0:T(8,128)(2,1)S(1)}, bf16[40,1024]{1,0:T(8,128)(2,1)S(1)}, u32[]{:S(2)}, u32[]{:S(2)}) collective-permute-start(bf16[40,1024]{1,0:T(8,128)(2,1)S(1)} %get-tuple-element.601), channel_id=1, source_target_pairs={{0,6},{1,7},{2,0},{3,1},{4,2},{5,3},{6,4},{7,5},{8,14},{9,15},{10,... | collective-permute-start | bytes 245768 | tf_op jit(solution)/shard_map/while/body/eval_jaxpr/ppermute | solution.py:39
  447.0 5.6 collective-permute-done.12.refs_2_
  460.7 5.4 collective-permute-start.3
  466.2 5.7 collective-permute-done.2
  476.4 6.0 %collective-permute-done.4.refs_5_ = bf16[160,1024]{1,0:T(8,128)(2,1)S(1)} collective-permute-done((bf16[160,1024]{1,0:T(8,128)(2,1)S(1)}, bf16[160,1024]{1,0:T(8,128)(2,1)S(1)}, u32[]{:S(2)}, u32[]{:S(2)}) %collective-permute-start.4) | collective-permute-done | bytes 327712 | tf_op jit(solution)/shard_map/while/body/eval_jaxpr/ppermute | solution.py:39
  510.1 8.7 %collective-permute-start.14 = (f32[128,1024]{1,0:T(8,128)S(1)}, f32[128,1024]{1,0:T(8,128)S(1)}, u32[]{:S(2)}, u32[]{:S(2)}) collective-permute-start(f32[128,1024]{1,0:T(8,128)S(1)} %eval_jaxpr.46), channel_id=1, source_target_pairs={{0,1},{1,0},{2,3},{3,2},{4,5},{5,4},{6,7},{7,6},{8,9},{9,8},{10,11... | collective-permute-start | bytes 1572872 | tf_op jit(solution)/shard_map/while/body/eval_jaxpr/ppermute | solution.py:44
  (384 shorter events, 424.2 us)
Async XLA Ops:
  1.0 12.8 %collective-permute-start.15 = (bf16[2,64,1024]{2,1,0:T(8,128)(2,1)S(1)}, bf16[2,64,1024]{2,1,0:T(8,128)(2,1)S(1)}, u32[]{:S(2)}, u32[]{:S(2)}) collective-permute-start(bf16[2,64,1024]{2,1,0:T(8,128)(2,1)S(1)} %constant_dynamic-slice_fusion.4), channel_id=1, source_target_pairs={{0,1},{1,0},{2,3},{3,2},{4,5},{5,4},{6,7},{7,6},{8,9},{9,8},{10,11... | collective-permute-start | bytes 786440 | tf_op jit(solution)/shard_map/ppermute | solution.py:44
  9.8 45.1 %collective-permute-start.16 = (bf16[384,1024]{1,0:T(8,128)(2,1)}, bf16[384,1024]{1,0:T(8,128)(2,1)}, u32[]{:S(2)}, u32[]{:S(2)}) collective-permute-start(bf16[384,1024]{1,0:T(8,128)(2,1)} %get-tuple-element.459), channel_id=1, source_target_pairs={{0,8},{8,16},{16,24},{24,0},{1,9},{9,17},{17,25},{25,1},{2,10},{10... | collective-permute-start | bytes 2359304 | tf_op jit(solution)/shard_map/ppermute | solution.py:39
  9.8 45.1 %collective-permute-start.17 = (bf16[384,1024]{1,0:T(8,128)(2,1)S(1)}, bf16[384,1024]{1,0:T(8,128)(2,1)}, u32[]{:S(2)}, u32[]{:S(2)}) collective-permute-start(bf16[384,1024]{1,0:T(8,128)(2,1)S(1)} %get-tuple-element.461), channel_id=1, source_target_pairs={{0,24},{8,0},{16,8},{24,16},{1,25},{9,1},{17,9},{25,17},{2,26},{10... | collective-permute-start | bytes 2359304 | tf_op jit(solution)/shard_map/ppermute | solution.py:39
  12.5 42.4 %collective-permute-start.18 = (bf16[384,1024]{1,0:T(8,128)(2,1)S(1)}, bf16[384,1024]{1,0:T(8,128)(2,1)}, u32[]{:S(2)}, u32[]{:S(2)}) collective-permute-start(bf16[384,1024]{1,0:T(8,128)(2,1)S(1)} %get-tuple-element.458), channel_id=1, source_target_pairs={{0,16},{8,24},{16,0},{24,8},{1,17},{9,25},{17,1},{25,9},{2,18},{10... | collective-permute-start | bytes 2359304 | tf_op jit(solution)/shard_map/ppermute | solution.py:39
  31.3 22.9 %collective-permute-start.23 = (bf16[160,1024]{1,0:T(8,128)(2,1)S(1)}, bf16[160,1024]{1,0:T(8,128)(2,1)S(1)}, u32[]{:S(2)}, u32[]{:S(2)}) collective-permute-start(bf16[160,1024]{1,0:T(8,128)(2,1)S(1)} %constant_dynamic-update-slice_fusion.4.refs_4_), channel_id=1, source_target_pairs={{0,8},{8,16},{16,24},{24,0},{1,9},{9,17},{17,25},{25,1},{2,10},{10... | collective-permute-start | bytes 983048 | tf_op jit(solution)/shard_map/ppermute | solution.py:39
  31.6 27.2 %collective-permute-start.24 = (bf16[160,1024]{1,0:T(8,128)(2,1)S(1)}, bf16[160,1024]{1,0:T(8,128)(2,1)S(1)}, u32[]{:S(2)}, u32[]{:S(2)}) collective-permute-start(bf16[160,1024]{1,0:T(8,128)(2,1)S(1)} %constant_dynamic-update-slice_fusion.4.refs_4_), channel_id=1, source_target_pairs={{0,24},{8,0},{16,8},{24,16},{1,25},{9,1},{17,9},{25,17},{2,26},{10... | collective-permute-start | bytes 983048 | tf_op jit(solution)/shard_map/ppermute | solution.py:39
  114.9 13.1 %collective-permute-start.7 = (bf16[128,1024]{1,0:T(8,128)(2,1)S(1)}, bf16[128,1024]{1,0:T(8,128)(2,1)S(1)}, u32[]{:S(2)}, u32[]{:S(2)}) collective-permute-start(bf16[128,1024]{1,0:T(8,128)(2,1)S(1)} %get-tuple-element.627.stream), channel_id=1, source_target_pairs={{0,32},{32,64},{64,96},{96,128},{128,160},{160,192},{192,224},{224... | collective-permute-start | bytes 786440 | tf_op jit(solution)/shard_map/while/body/eval_jaxpr/ppermute | solution.py:39
  175.8 13.8 %collective-permute-start.6 = (bf16[160,1024]{1,0:T(8,128)(2,1)S(1)}, bf16[160,1024]{1,0:T(8,128)(2,1)S(1)}, u32[]{:S(2)}, u32[]{:S(2)}) collective-permute-start(bf16[160,1024]{1,0:T(8,128)(2,1)S(1)} %constant_dynamic-update-slice_fusion.15.refs_4_), channel_id=1, source_target_pairs={{0,16},{8,24},{16,0},{24,8},{1,17},{9,25},{17,1},{25,9},{2,18},{10... | collective-permute-start | bytes 983048 | tf_op jit(solution)/shard_map/while/body/eval_jaxpr/ppermute | solution.py:39
  176.4 14.2 %collective-permute-start.7 = (bf16[128,1024]{1,0:T(8,128)(2,1)S(1)}, bf16[128,1024]{1,0:T(8,128)(2,1)S(1)}, u32[]{:S(2)}, u32[]{:S(2)}) collective-permute-start(bf16[128,1024]{1,0:T(8,128)(2,1)S(1)} %get-tuple-element.627.stream), channel_id=1, source_target_pairs={{0,32},{32,64},{64,96},{96,128},{128,160},{160,192},{192,224},{224... | collective-permute-start | bytes 786440 | tf_op jit(solution)/shard_map/while/body/eval_jaxpr/ppermute | solution.py:39
  235.6 14.2 %collective-permute-start.6 = (bf16[160,1024]{1,0:T(8,128)(2,1)S(1)}, bf16[160,1024]{1,0:T(8,128)(2,1)S(1)}, u32[]{:S(2)}, u32[]{:S(2)}) collective-permute-start(bf16[160,1024]{1,0:T(8,128)(2,1)S(1)} %constant_dynamic-update-slice_fusion.15.refs_4_), channel_id=1, source_target_pairs={{0,16},{8,24},{16,0},{24,8},{1,17},{9,25},{17,1},{25,9},{2,18},{10... | collective-permute-start | bytes 983048 | tf_op jit(solution)/shard_map/while/body/eval_jaxpr/ppermute | solution.py:39
  236.7 14.0 %collective-permute-start.7 = (bf16[128,1024]{1,0:T(8,128)(2,1)S(1)}, bf16[128,1024]{1,0:T(8,128)(2,1)S(1)}, u32[]{:S(2)}, u32[]{:S(2)}) collective-permute-start(bf16[128,1024]{1,0:T(8,128)(2,1)S(1)} %get-tuple-element.627.stream), channel_id=1, source_target_pairs={{0,32},{32,64},{64,96},{96,128},{128,160},{160,192},{192,224},{224... | collective-permute-start | bytes 786440 | tf_op jit(solution)/shard_map/while/body/eval_jaxpr/ppermute | solution.py:39
  296.8 13.7 %collective-permute-start.6 = (bf16[160,1024]{1,0:T(8,128)(2,1)S(1)}, bf16[160,1024]{1,0:T(8,128)(2,1)S(1)}, u32[]{:S(2)}, u32[]{:S(2)}) collective-permute-start(bf16[160,1024]{1,0:T(8,128)(2,1)S(1)} %constant_dynamic-update-slice_fusion.15.refs_4_), channel_id=1, source_target_pairs={{0,16},{8,24},{16,0},{24,8},{1,17},{9,25},{17,1},{25,9},{2,18},{10... | collective-permute-start | bytes 983048 | tf_op jit(solution)/shard_map/while/body/eval_jaxpr/ppermute | solution.py:39
  297.6 13.8 %collective-permute-start.7 = (bf16[128,1024]{1,0:T(8,128)(2,1)S(1)}, bf16[128,1024]{1,0:T(8,128)(2,1)S(1)}, u32[]{:S(2)}, u32[]{:S(2)}) collective-permute-start(bf16[128,1024]{1,0:T(8,128)(2,1)S(1)} %get-tuple-element.627.stream), channel_id=1, source_target_pairs={{0,32},{32,64},{64,96},{96,128},{128,160},{160,192},{192,224},{224... | collective-permute-start | bytes 786440 | tf_op jit(solution)/shard_map/while/body/eval_jaxpr/ppermute | solution.py:39
  354.2 13.1 %collective-permute-start.5 = (bf16[160,1024]{1,0:T(8,128)(2,1)S(1)}, bf16[160,1024]{1,0:T(8,128)(2,1)S(1)}, u32[]{:S(2)}, u32[]{:S(2)}) collective-permute-start(bf16[160,1024]{1,0:T(8,128)(2,1)S(1)} %constant_dynamic-update-slice_fusion.15.refs_4_), channel_id=1, source_target_pairs={{0,24},{8,0},{16,8},{24,16},{1,25},{9,1},{17,9},{25,17},{2,26},{10... | collective-permute-start | bytes 983048 | tf_op jit(solution)/shard_map/while/body/eval_jaxpr/ppermute | solution.py:39
  399.8 12.8 %collective-permute-start.2 = (bf16[40,1024]{1,0:T(8,128)(2,1)S(1)}, bf16[40,1024]{1,0:T(8,128)(2,1)S(1)}, u32[]{:S(2)}, u32[]{:S(2)}) collective-permute-start(bf16[40,1024]{1,0:T(8,128)(2,1)S(1)} %get-tuple-element.591), channel_id=1, source_target_pairs={{0,36},{1,37},{2,38},{3,39},{4,32},{5,33},{6,34},{7,35},{32,68},{3... | collective-permute-start | bytes 245768 | tf_op jit(solution)/shard_map/while/body/eval_jaxpr/ppermute | solution.py:54
  412.7 15.2 %collective-permute-start.5 = (bf16[160,1024]{1,0:T(8,128)(2,1)S(1)}, bf16[160,1024]{1,0:T(8,128)(2,1)S(1)}, u32[]{:S(2)}, u32[]{:S(2)}) collective-permute-start(bf16[160,1024]{1,0:T(8,128)(2,1)S(1)} %constant_dynamic-update-slice_fusion.15.refs_4_), channel_id=1, source_target_pairs={{0,24},{8,0},{16,8},{24,16},{1,25},{9,1},{17,9},{25,17},{2,26},{10... | collective-permute-start | bytes 983048 | tf_op jit(solution)/shard_map/while/body/eval_jaxpr/ppermute | solution.py:39
  415.4 13.5 %collective-permute-start.7 = (bf16[128,1024]{1,0:T(8,128)(2,1)S(1)}, bf16[128,1024]{1,0:T(8,128)(2,1)S(1)}, u32[]{:S(2)}, u32[]{:S(2)}) collective-permute-start(bf16[128,1024]{1,0:T(8,128)(2,1)S(1)} %get-tuple-element.627.stream), channel_id=1, source_target_pairs={{0,32},{32,64},{64,96},{96,128},{128,160},{160,192},{192,224},{224... | collective-permute-start | bytes 786440 | tf_op jit(solution)/shard_map/while/body/eval_jaxpr/ppermute | solution.py:39
  459.1 12.8 %collective-permute-start.2 = (bf16[40,1024]{1,0:T(8,128)(2,1)S(1)}, bf16[40,1024]{1,0:T(8,128)(2,1)S(1)}, u32[]{:S(2)}, u32[]{:S(2)}) collective-permute-start(bf16[40,1024]{1,0:T(8,128)(2,1)S(1)} %get-tuple-element.591), channel_id=1, source_target_pairs={{0,36},{1,37},{2,38},{3,39},{4,32},{5,33},{6,34},{7,35},{32,68},{3... | collective-permute-start | bytes 245768 | tf_op jit(solution)/shard_map/while/body/eval_jaxpr/ppermute | solution.py:54
  472.6 13.7 %collective-permute-start.5 = (bf16[160,1024]{1,0:T(8,128)(2,1)S(1)}, bf16[160,1024]{1,0:T(8,128)(2,1)S(1)}, u32[]{:S(2)}, u32[]{:S(2)}) collective-permute-start(bf16[160,1024]{1,0:T(8,128)(2,1)S(1)} %constant_dynamic-update-slice_fusion.15.refs_4_), channel_id=1, source_target_pairs={{0,24},{8,0},{16,8},{24,16},{1,25},{9,1},{17,9},{25,17},{2,26},{10... | collective-permute-start | bytes 983048 | tf_op jit(solution)/shard_map/while/body/eval_jaxpr/ppermute | solution.py:39
  475.3 15.0 %collective-permute-start.6 = (bf16[160,1024]{1,0:T(8,128)(2,1)S(1)}, bf16[160,1024]{1,0:T(8,128)(2,1)S(1)}, u32[]{:S(2)}, u32[]{:S(2)}) collective-permute-start(bf16[160,1024]{1,0:T(8,128)(2,1)S(1)} %constant_dynamic-update-slice_fusion.15.refs_4_), channel_id=1, source_target_pairs={{0,16},{8,24},{16,0},{24,8},{1,17},{9,25},{17,1},{25,9},{2,18},{10... | collective-permute-start | bytes 983048 | tf_op jit(solution)/shard_map/while/body/eval_jaxpr/ppermute | solution.py:39
  476.3 14.9 %collective-permute-start.7 = (bf16[128,1024]{1,0:T(8,128)(2,1)S(1)}, bf16[128,1024]{1,0:T(8,128)(2,1)S(1)}, u32[]{:S(2)}, u32[]{:S(2)}) collective-permute-start(bf16[128,1024]{1,0:T(8,128)(2,1)S(1)} %get-tuple-element.627.stream), channel_id=1, source_target_pairs={{0,32},{32,64},{64,96},{96,128},{128,160},{160,192},{192,224},{224... | collective-permute-start | bytes 786440 | tf_op jit(solution)/shard_map/while/body/eval_jaxpr/ppermute | solution.py:39
  533.1 13.0 %collective-permute-start.5 = (bf16[160,1024]{1,0:T(8,128)(2,1)S(1)}, bf16[160,1024]{1,0:T(8,128)(2,1)S(1)}, u32[]{:S(2)}, u32[]{:S(2)}) collective-permute-start(bf16[160,1024]{1,0:T(8,128)(2,1)S(1)} %constant_dynamic-update-slice_fusion.15.refs_4_), channel_id=1, source_target_pairs={{0,24},{8,0},{16,8},{24,16},{1,25},{9,1},{17,9},{25,17},{2,26},{10... | collective-permute-start | bytes 983048 | tf_op jit(solution)/shard_map/while/body/eval_jaxpr/ppermute | solution.py:39
  535.8 14.6 %collective-permute-start.6 = (bf16[160,1024]{1,0:T(8,128)(2,1)S(1)}, bf16[160,1024]{1,0:T(8,128)(2,1)S(1)}, u32[]{:S(2)}, u32[]{:S(2)}) collective-permute-start(bf16[160,1024]{1,0:T(8,128)(2,1)S(1)} %constant_dynamic-update-slice_fusion.15.refs_4_), channel_id=1, source_target_pairs={{0,16},{8,24},{16,0},{24,8},{1,17},{9,25},{17,1},{25,9},{2,18},{10... | collective-permute-start | bytes 983048 | tf_op jit(solution)/shard_map/while/body/eval_jaxpr/ppermute | solution.py:39
  536.7 14.7 %collective-permute-start.7 = (bf16[128,1024]{1,0:T(8,128)(2,1)S(1)}, bf16[128,1024]{1,0:T(8,128)(2,1)S(1)}, u32[]{:S(2)}, u32[]{:S(2)}) collective-permute-start(bf16[128,1024]{1,0:T(8,128)(2,1)S(1)} %get-tuple-element.627.stream), channel_id=1, source_target_pairs={{0,32},{32,64},{64,96},{96,128},{128,160},{160,192},{192,224},{224... | collective-permute-start | bytes 786440 | tf_op jit(solution)/shard_map/while/body/eval_jaxpr/ppermute | solution.py:39
  (118 other events, 922.9 us)

commit v2 on v1

--- a/solution.py
+++ b/solution.py
@@ -16,6 +16,7 @@
 HBM = pl.BlockSpec(memory_space=pltpu.HBM)
 CHIP_SHIFTS = (2, 1, 3)
 RANK_SHIFTS = (2, 1, 3)
+BLOCK_PAIRS = ((2, 1), (3, 0))
 
 
 def kernel_call(body, in_specs, out_shapes, mib, scratch=(), flops=0, moved=0):
@@ -115,10 +116,18 @@
     out[...] = update + jnp.dot(low[which[0]], rows, preferred_element_type=f32)
 
 
+def joined(halves, i):
+    return jnp.concatenate([halves[2 * i][...], halves[2 * i + 1][...]]).astype(f32)
+
+
+def marker_kernel(which, gains, out):
+    out[...] = gains[...]
+
+
 def gate_up_first(early, late, rank, gains, w_gate, w_up, *refs):
     count, downs = len(early), len(early) + len(late)
     w_down, refs = refs[:downs], refs[downs:]
-    slices, refs = refs[:count], refs[count:]
+    slices, refs = refs[: 2 * count], refs[2 * count :]
     gate_out, up_out, squares_out, gate_late, up_late, down_out, gate_buf, up_buf, sems, late_sems, down_sems = refs
     width = slices[0].shape[1]
     ranks = w_gate.shape[0] // width
@@ -137,7 +146,7 @@
         copy.start()
     gate, up, squares = 0.0, 0.0, 0.0
     for i, k in enumerate(early):
-        wide = slices[i][...].astype(f32)
+        wide = joined(slices, i)
         squares = squares + jnp.sum(wide * wide, axis=1, keepdims=True)
         scaled = (wide * gains[k : k + 1]).astype(bf16)
         now[i][0].wait()
@@ -155,7 +164,7 @@
     *slices, hidden = refs
     gate, up, squares = gate_in[...], up_in[...], squares_in[:, :1]
     for i, k in enumerate(late):
-        wide = slices[i][...].astype(f32)
+        wide = joined(slices, i)
         squares = squares + jnp.sum(wide * wide, axis=1, keepdims=True)
         scaled = (wide * gains[k : k + 1]).astype(bf16)
         gate = gate + jnp.dot(scaled, gate_late[i], preferred_element_type=f32)
@@ -234,7 +243,7 @@
     early, late = (0, 1), (3, 2)
     gate_up_a = kernel_call(
         functools.partial(gate_up_first, early, late),
-        (SMEM, VMEM, HBM, HBM) + (HBM,) * ranks + (VMEM,) * 2,
+        (SMEM, VMEM, HBM, HBM) + (HBM,) * ranks + (VMEM,) * 4,
         (shape(rows, hidden_width, kind=f32),) * 2
         + (shape(rows, 128, kind=f32),)
         + (shape(2, width, hidden_width),) * 2
@@ -245,7 +254,7 @@
         flops=3 * 10**9,
     )
     gate_up_b = kernel_call(
-        functools.partial(gate_up_last, late, model_width), (VMEM,) * 8, shape(rows, hidden_width), 16, flops=10**9
+        functools.partial(gate_up_last, late, model_width), (VMEM,) * 10, shape(rows, hidden_width), 16, flops=10**9
     )
     down_a = kernel_call(down_first, (VMEM,) * 3, shape(rows, width, kind=f32), 16, flops=5 * 10**8)
     down_b = kernel_call(down_last, (VMEM,) * 4, (shape(per_chip, width),) * chips, 16, flops=5 * 10**8)
@@ -253,20 +262,24 @@
     rank_word = rank.reshape(1).astype(i32)
     gain_parts = jnp.concatenate([slice_at(gains, rank - k, 1) for k in range(ranks)])
 
-    def expert_work(blocks, down_parts, also):
-        own = jnp.concatenate(blocks)
-        slices = {k: shifted(own, "tensor", k) for k in RANK_SHIFTS}
-        slices[0] = own
+    marker = kernel_call(marker_kernel, (SMEM, VMEM), shape(ranks, width, kind=f32), 4, flops=10**6)
+
+    def expert_work(blocks, down_parts, also, gain_parts):
+        halves = [jnp.concatenate([blocks[k] for k in pair]) for pair in BLOCK_PAIRS]
+        slices = {k: [shifted(half, "tensor", k) for half in halves] for k in RANK_SHIFTS}
+        slices[0] = halves
         weights = [in_hbm(value) for value in (gate_matrix, up_matrix, *(down_parts[k] for k in (*early, *late)))]
         gate, up, squares, gate_late, up_late, matrices = gate_up_a(
-            rank_word, gain_parts, *weights, *(slices[k] for k in early)
+            rank_word, gain_parts, *weights, *(half for k in early for half in slices[k])
         )
-        hidden = gate_up_b(gain_parts, gate_late, up_late, gate, up, squares, *(slices[k] for k in late))
+        hidden = gate_up_b(gain_parts, gate_late, up_late, gate, up, squares, *(half for k in late for half in slices[k]))
         hidden, also = lax.optimization_barrier((hidden, also))
         hiddens = {k: shifted(hidden, "tensor", k) for k in RANK_SHIFTS}
         hiddens[0] = hidden
         total = down_a(matrices, *(hiddens[k] for k in early))
-        return down_b(matrices, total, *(hiddens[k] for k in late)), also
+        outs = down_b(matrices, total, *(hiddens[k] for k in late))
+        order = [k for pair in BLOCK_PAIRS for k in pair]
+        return [outs[order.index(k)] for k in range(chips)], also
 
     def to_home(blocks):
         back = {k: shifted(blocks[k], "expert", groups - 2 * k) for k in CHIP_SHIFTS}
@@ -290,7 +303,7 @@
     next_info = shifted(info, "pipe", sections - 1)
     place = tables(where, next_info)[0]
 
-    blocks, stream = expert_work([moved[k] for k in range(chips)], down_parts, entering[0])
+    blocks, stream = expert_work([moved[k] for k in range(chips)], down_parts, entering[0], gain_parts)
     fresh = combined(stream, to_home(blocks), jnp.zeros((), i32))
     collected = kept(jnp.zeros((micro_count, local_tokens, width), bf16), fresh, 0)
     fresh = jnp.where(section == sections - 1, entering[1], fresh)
@@ -302,7 +315,9 @@
         outgoing = dispatch(leaving.reshape(1), place, fresh)
         moved = {k: onward(outgoing[k], k) for k in (*CHIP_SHIFTS, 0)}
         stream = shifted(fresh, "pipe", 1)
-        blocks, stream = expert_work([moved[k] for k in range(chips)], down_parts, stream)
+        gains_here = marker(index.reshape(1), gain_parts)
+        gains_here = marker(index.reshape(1), gains_here)
+        blocks, stream = expert_work([moved[k] for k in range(chips)], down_parts, stream, gains_here)
         fresh = combined(stream, to_home(blocks), jnp.clip(unit, 0, micro_count - 1))
         return fresh, kept(collected, fresh, jnp.clip(unit, 0, micro_count))
 

time: 580 us -> 590 us (1.017)
  starting transfers between devices: 253 us -> 302 us
  waiting for transfers between devices: 255 us -> 214 us
    ppermute x96 -> x123, waiting for transfers between devices: 192 us -> 159 us  [shifted(): lax.ppermute(block, axis, [(i, (i + distance) % size) for i in range(size)])]
    ppermute x11, starting transfers between devices: 40.3 us -> 60.4 us  [core_swap(): return lax.ppermute(block, 'expert', [(i, i ^ 1) for i in range(size)])]
    ppermute x32, starting transfers between devices: 51.8 us -> 70.2 us  [onward(): return lax.ppermute(block, ('pipe', 'expert'), route)]
    ppermute x96 -> x123, starting transfers between devices: 161 us -> 171 us  [shifted(): lax.ppermute(block, axis, [(i, (i + distance) % size) for i in range(size)])]
    ppermute x32, waiting for transfers between devices: 50.7 us -> 42.3 us  [onward(): return lax.ppermute(block, ('pipe', 'expert'), route)]
    pallas_call x27 -> x43, Pallas kernels: 48.1 us -> 49.8 us  [the longest x9 37.6 us: expert_work(): gate_up_a(rank_word, gain_parts, *weights, *(half for k in early for half...]
  transfers between devices with their start and end apart: 139 -> 166, of which waited for: 90 -> 93; matrix products, arithmetic and copies ran while one was open for 1% -> 1% of each run, Pallas kernels for 9% -> 9%
where the time goes in v2:
time: 590 us
  starting transfers between devices  302 us (51%)
  waiting for transfers between devices  214 us (36%)
  Pallas kernels  62.3 us (11%)
    ppermute x123, starting transfers between devices, shifted(): lax.ppermute(block, axis, [(i, (i + distance) % size) for i in range(size)])  171 us
    ppermute x123, waiting for transfers between devices, shifted(): lax.ppermute(block, axis, [(i, (i + distance) % size) for i in range(size)])  159 us
    ppermute x32, starting transfers between devices, onward(): return lax.ppermute(block, ('pipe', 'expert'), route)  70.2 us
    ppermute x11, starting transfers between devices, core_swap(): return lax.ppermute(block, 'expert', [(i, i ^ 1) for i in range(size)])  60.4 us
    ppermute x32, waiting for transfers between devices, onward(): return lax.ppermute(block, ('pipe', 'expert'), route)  42.3 us
    pallas_call x9, Pallas kernels, expert_work(): gate_up_a(rank_word, gain_parts, *weights, *(half for k in early for half...  37.6 us
    ppermute x11, waiting for transfers between devices, core_swap(): return lax.ppermute(block, 'expert', [(i, i ^ 1) for i in range(size)])  12.3 us
  transfers between devices with their start and end apart: 166, of which 93 were waited for; matrix products, arithmetic and copies ran while one was open for 1% of the time, Pallas kernels for 9%

profile of v2, /device:TPU:1, one launch (start us, length us, event | category | flops | bytes accessed | tf_op | source)
XLA Modules:
  0.0 590.0 jit_solution(8227641248154676991)
XLA Ops:
  15.2 7.0 %collective-permute-start.23 = (bf16[40,1024]{1,0:T(8,128)(2,1)S(1)}, bf16[40,1024]{1,0:T(8,128)(2,1)S(1)}, u32[]{:S(2)}, u32[]{:S(2)}) collective-permute-start(bf16[40,1024]{1,0:T(8,128)(2,1)S(1)} %get-tuple-element.402), channel_id=1, source_target_pairs={{0,4},{1,5},{2,6},{3,7},{4,0},{5,1},{6,2},{7,3},{8,12},{9,13},{10,... | collective-permute-start | bytes 245768 | tf_op jit(solution)/shard_map/ppermute | solution.py:40
  24.1 4.6 collective-permute-start.25
  30.7 20.1 %collective-permute-done.26.refs_6_ = bf16[80,1024]{1,0:T(8,128)(2,1)S(1)} collective-permute-done((bf16[80,1024]{1,0:T(8,128)(2,1)S(1)}, bf16[80,1024]{1,0:T(8,128)(2,1)S(1)}, u32[]{:S(2)}, u32[]{:S(2)}) %collective-permute-start.26) | collective-permute-done | bytes 163872 | tf_op jit(solution)/shard_map/ppermute | solution.py:40
  75.9 6.1 %collective-permute-start.35 = (bf16[40,1024]{1,0:T(8,128)(2,1)S(1)}, bf16[40,1024]{1,0:T(8,128)(2,1)S(1)}, u32[]{:S(2)}, u32[]{:S(2)}) collective-permute-start(bf16[40,1024]{1,0:T(8,128)(2,1)S(1)} %get-tuple-element.417), channel_id=1, source_target_pairs={{0,6},{1,7},{2,0},{3,1},{4,2},{5,3},{6,4},{7,5},{8,14},{9,15},{10,... | collective-permute-start | bytes 245768 | tf_op jit(solution)/shard_map/ppermute | solution.py:40
  100.9 488.5 %while.17 = (s32[]{:T(128)}, bf16[128,1024]{1,0:T(8,128)(2,1)S(1)}, bf16[2,64,1024]{2,1,0:T(8,128)(2,1)S(1)}, f32[4,1024]{1,0:T(4,128)S(1)}, s32[]{:T(128)}, /*i...) while((s32[]{:T(128)}, bf16[128,1024]{1,0:T(8,128)(2,1)S(1)}, ...), condition=%wide.region_1.2_spmd, body=%wide.region_0.1_spmd.sunk | while | flops 7002589696 | bytes 13468684 | solution.py:324
  108.8 5.6 collective-permute-done.3
  140.0 4.7 collective-permute-start.15
  150.3 6.2 %collective-permute-start.17 = (f32[128,1024]{1,0:T(8,128)S(1)}, f32[128,1024]{1,0:T(8,128)S(1)}, u32[]{:S(2)}, u32[]{:S(2)}) collective-permute-start(f32[128,1024]{1,0:T(8,128)S(1)} %eval_jaxpr.50), channel_id=1, source_target_pairs={{0,1},{1,0},{2,3},{3,2},{4,5},{5,4},{6,7},{7,6},{8,9},{9,8},{10,11... | collective-permute-start | bytes 1572872 | tf_op jit(solution)/shard_map/while/body/eval_jaxpr/ppermute | solution.py:45
  164.3 5.7 collective-permute-start.1
  226.4 4.5 collective-permute-start.1
  270.7 10.5 %collective-permute-start.17 = (f32[128,1024]{1,0:T(8,128)S(1)}, f32[128,1024]{1,0:T(8,128)S(1)}, u32[]{:S(2)}, u32[]{:S(2)}) collective-permute-start(f32[128,1024]{1,0:T(8,128)S(1)} %eval_jaxpr.50), channel_id=1, source_target_pairs={{0,1},{1,0},{2,3},{3,2},{4,5},{5,4},{6,7},{7,6},{8,9},{9,8},{10,11... | collective-permute-start | bytes 1572872 | tf_op jit(solution)/shard_map/while/body/eval_jaxpr/ppermute | solution.py:45
  287.0 4.7 collective-permute-start.1
  301.4 5.1 collective-permute-done.4.refs_6_
  323.4 6.5 %collective-permute-start.15 = (bf16[40,1024]{1,0:T(8,128)(2,1)S(1)}, bf16[40,1024]{1,0:T(8,128)(2,1)S(1)}, u32[]{:S(2)}, u32[]{:S(2)}) collective-permute-start(bf16[40,1024]{1,0:T(8,128)(2,1)S(1)} %get-tuple-element.602), channel_id=1, source_target_pairs={{0,4},{1,5},{2,6},{3,7},{4,0},{5,1},{6,2},{7,3},{8,12},{9,13},{10,... | collective-permute-start | bytes 245768 | tf_op jit(solution)/shard_map/while/body/eval_jaxpr/ppermute | solution.py:40
  335.8 5.6 collective-permute-start.17
  347.5 4.9 collective-permute-start.1
  385.3 4.9 collective-permute-start.15
  396.0 6.9 %collective-permute-start.17 = (f32[128,1024]{1,0:T(8,128)S(1)}, f32[128,1024]{1,0:T(8,128)S(1)}, u32[]{:S(2)}, u32[]{:S(2)}) collective-permute-start(f32[128,1024]{1,0:T(8,128)S(1)} %eval_jaxpr.50), channel_id=1, source_target_pairs={{0,1},{1,0},{2,3},{3,2},{4,5},{5,4},{6,7},{7,6},{8,9},{9,8},{10,11... | collective-permute-start | bytes 1572872 | tf_op jit(solution)/shard_map/while/body/eval_jaxpr/ppermute | solution.py:45
  452.9 4.8 collective-permute-done.15.refs_2_
  474.0 5.9 %collective-permute-done.3 = bf16[40,1024]{1,0:T(8,128)(2,1)S(1)} collective-permute-done((bf16[40,1024]{1,0:T(8,128)(2,1)S(1)}, bf16[40,1024]{1,0:T(8,128)(2,1)S(1)}, u32[]{:S(2)}, u32[]{:S(2)}) %collective-permute-start.3) | collective-permute-done | bytes 81952 | tf_op jit(solution)/shard_map/while/body/eval_jaxpr/ppermute | solution.py:55
  517.0 10.3 %collective-permute-start.17 = (f32[128,1024]{1,0:T(8,128)S(1)}, f32[128,1024]{1,0:T(8,128)S(1)}, u32[]{:S(2)}, u32[]{:S(2)}) collective-permute-start(f32[128,1024]{1,0:T(8,128)S(1)} %eval_jaxpr.50), channel_id=1, source_target_pairs={{0,1},{1,0},{2,3},{3,2},{4,5},{5,4},{6,7},{7,6},{8,9},{9,8},{10,11... | collective-permute-start | bytes 1572872 | tf_op jit(solution)/shard_map/while/body/eval_jaxpr/ppermute | solution.py:45
  530.0 4.8 collective-permute-start.1
  568.2 6.0 %collective-permute-start.15 = (bf16[40,1024]{1,0:T(8,128)(2,1)S(1)}, bf16[40,1024]{1,0:T(8,128)(2,1)S(1)}, u32[]{:S(2)}, u32[]{:S(2)}) collective-permute-start(bf16[40,1024]{1,0:T(8,128)(2,1)S(1)} %get-tuple-element.602), channel_id=1, source_target_pairs={{0,4},{1,5},{2,6},{3,7},{4,0},{5,1},{6,2},{7,3},{8,12},{9,13},{10,... | collective-permute-start | bytes 245768 | tf_op jit(solution)/shard_map/while/body/eval_jaxpr/ppermute | solution.py:40
  580.7 6.9 %collective-permute-start.17 = (f32[128,1024]{1,0:T(8,128)S(1)}, f32[128,1024]{1,0:T(8,128)S(1)}, u32[]{:S(2)}, u32[]{:S(2)}) collective-permute-start(f32[128,1024]{1,0:T(8,128)S(1)} %eval_jaxpr.50), channel_id=1, source_target_pairs={{0,1},{1,0},{2,3},{3,2},{4,5},{5,4},{6,7},{7,6},{8,9},{9,8},{10,11... | collective-permute-start | bytes 1572872 | tf_op jit(solution)/shard_map/while/body/eval_jaxpr/ppermute | solution.py:45
  (454 shorter events, 436.0 us)
Async XLA Ops:
  1.0 12.9 %collective-permute-start.18 = (bf16[2,64,1024]{2,1,0:T(8,128)(2,1)S(1)}, bf16[2,64,1024]{2,1,0:T(8,128)(2,1)S(1)}, u32[]{:S(2)}, u32[]{:S(2)}) collective-permute-start(bf16[2,64,1024]{2,1,0:T(8,128)(2,1)S(1)} %constant_dynamic-slice_fusion.4), channel_id=1, source_target_pairs={{0,1},{1,0},{2,3},{3,2},{4,5},{5,4},{6,7},{7,6},{8,9},{9,8},{10,11... | collective-permute-start | bytes 786440 | tf_op jit(solution)/shard_map/ppermute | solution.py:45
  9.8 45.1 %collective-permute-start.19 = (bf16[384,1024]{1,0:T(8,128)(2,1)}, bf16[384,1024]{1,0:T(8,128)(2,1)}, u32[]{:S(2)}, u32[]{:S(2)}) collective-permute-start(bf16[384,1024]{1,0:T(8,128)(2,1)} %get-tuple-element.459), channel_id=1, source_target_pairs={{0,8},{8,16},{16,24},{24,0},{1,9},{9,17},{17,25},{25,1},{2,10},{10... | collective-permute-start | bytes 2359304 | tf_op jit(solution)/shard_map/ppermute | solution.py:40
  9.8 45.5 %collective-permute-start.20 = (bf16[384,1024]{1,0:T(8,128)(2,1)S(1)}, bf16[384,1024]{1,0:T(8,128)(2,1)}, u32[]{:S(2)}, u32[]{:S(2)}) collective-permute-start(bf16[384,1024]{1,0:T(8,128)(2,1)S(1)} %get-tuple-element.461), channel_id=1, source_target_pairs={{0,24},{8,0},{16,8},{24,16},{1,25},{9,1},{17,9},{25,17},{2,26},{10... | collective-permute-start | bytes 2359304 | tf_op jit(solution)/shard_map/ppermute | solution.py:40
  12.6 45.0 %collective-permute-start.21 = (bf16[384,1024]{1,0:T(8,128)(2,1)S(1)}, bf16[384,1024]{1,0:T(8,128)(2,1)}, u32[]{:S(2)}, u32[]{:S(2)}) collective-permute-start(bf16[384,1024]{1,0:T(8,128)(2,1)S(1)} %get-tuple-element.458), channel_id=1, source_target_pairs={{0,16},{8,24},{16,0},{24,8},{1,17},{9,25},{17,1},{25,9},{2,18},{10... | collective-permute-start | bytes 2359304 | tf_op jit(solution)/shard_map/ppermute | solution.py:40
  28.7 22.1 %collective-permute-start.26 = (bf16[80,1024]{1,0:T(8,128)(2,1)S(1)}, bf16[80,1024]{1,0:T(8,128)(2,1)S(1)}, u32[]{:S(2)}, u32[]{:S(2)}) collective-permute-start(bf16[80,1024]{1,0:T(8,128)(2,1)S(1)} %constant_dynamic-update-slice_fusion.4.refs_4_), channel_id=1, source_target_pairs={{0,8},{8,16},{16,24},{24,0},{1,9},{9,17},{17,25},{25,1},{2,10},{10... | collective-permute-start | bytes 491528 | tf_op jit(solution)/shard_map/ppermute | solution.py:40
  30.2 24.1 %collective-permute-start.27 = (bf16[80,1024]{1,0:T(8,128)(2,1)S(1)}, bf16[80,1024]{1,0:T(8,128)(2,1)S(1)}, u32[]{:S(2)}, u32[]{:S(2)}) collective-permute-start(bf16[80,1024]{1,0:T(8,128)(2,1)S(1)} %constant_dynamic-update-slice_fusion.6.refs_5_), channel_id=1, source_target_pairs={{0,8},{8,16},{16,24},{24,0},{1,9},{9,17},{17,25},{25,1},{2,10},{10... | collective-permute-start | bytes 491528 | tf_op jit(solution)/shard_map/ppermute | solution.py:40
  102.6 11.8 %collective-permute-start.3 = (bf16[40,1024]{1,0:T(8,128)(2,1)S(1)}, bf16[40,1024]{1,0:T(8,128)(2,1)S(1)}, u32[]{:S(2)}, u32[]{:S(2)}) collective-permute-start(bf16[40,1024]{1,0:T(8,128)(2,1)S(1)} %get-tuple-element.592), channel_id=1, source_target_pairs={{0,32},{1,33},{2,34},{3,35},{4,36},{5,37},{6,38},{7,39},{32,64},{3... | collective-permute-start | bytes 245768 | tf_op jit(solution)/shard_map/while/body/eval_jaxpr/ppermute | solution.py:55
  114.5 16.9 %collective-permute-start.10 = (bf16[128,1024]{1,0:T(8,128)(2,1)S(1)}, bf16[128,1024]{1,0:T(8,128)(2,1)S(1)}, u32[]{:S(2)}, u32[]{:S(2)}) collective-permute-start(bf16[128,1024]{1,0:T(8,128)(2,1)S(1)} %get-tuple-element.627.stream), channel_id=1, source_target_pairs={{0,32},{32,64},{64,96},{96,128},{128,160},{160,192},{192,224},{224... | collective-permute-start | bytes 786440 | tf_op jit(solution)/shard_map/while/body/eval_jaxpr/ppermute | solution.py:40
  114.6 13.2 %collective-permute-start.7 = (bf16[80,1024]{1,0:T(8,128)(2,1)S(1)}, bf16[80,1024]{1,0:T(8,128)(2,1)S(1)}, u32[]{:S(2)}, u32[]{:S(2)}) collective-permute-start(bf16[80,1024]{1,0:T(8,128)(2,1)S(1)} %constant_dynamic-update-slice_fusion.15.refs_5_), channel_id=1, source_target_pairs={{0,24},{8,0},{16,8},{24,16},{1,25},{9,1},{17,9},{25,17},{2,26},{10... | collective-permute-start | bytes 491528 | tf_op jit(solution)/shard_map/while/body/eval_jaxpr/ppermute | solution.py:40
  175.1 14.8 %collective-permute-start.10 = (bf16[128,1024]{1,0:T(8,128)(2,1)S(1)}, bf16[128,1024]{1,0:T(8,128)(2,1)S(1)}, u32[]{:S(2)}, u32[]{:S(2)}) collective-permute-start(bf16[128,1024]{1,0:T(8,128)(2,1)S(1)} %get-tuple-element.627.stream), channel_id=1, source_target_pairs={{0,32},{32,64},{64,96},{96,128},{128,160},{160,192},{192,224},{224... | collective-permute-start | bytes 786440 | tf_op jit(solution)/shard_map/while/body/eval_jaxpr/ppermute | solution.py:40
  217.9 13.0 %collective-permute-start.2 = (bf16[40,1024]{1,0:T(8,128)(2,1)S(1)}, bf16[40,1024]{1,0:T(8,128)(2,1)S(1)}, u32[]{:S(2)}, u32[]{:S(2)}) collective-permute-start(bf16[40,1024]{1,0:T(8,128)(2,1)S(1)} %get-tuple-element.591), channel_id=1, source_target_pairs={{0,38},{1,39},{2,32},{3,33},{4,34},{5,35},{6,36},{7,37},{32,70},{3... | collective-permute-start | bytes 245768 | tf_op jit(solution)/shard_map/while/body/eval_jaxpr/ppermute | solution.py:55
  237.0 14.7 %collective-permute-start.10 = (bf16[128,1024]{1,0:T(8,128)(2,1)S(1)}, bf16[128,1024]{1,0:T(8,128)(2,1)S(1)}, u32[]{:S(2)}, u32[]{:S(2)}) collective-permute-start(bf16[128,1024]{1,0:T(8,128)(2,1)S(1)} %get-tuple-element.627.stream), channel_id=1, source_target_pairs={{0,32},{32,64},{64,96},{96,128},{128,160},{160,192},{192,224},{224... | collective-permute-start | bytes 786440 | tf_op jit(solution)/shard_map/while/body/eval_jaxpr/ppermute | solution.py:40
  270.7 12.0 %collective-permute-start.17 = (f32[128,1024]{1,0:T(8,128)S(1)}, f32[128,1024]{1,0:T(8,128)S(1)}, u32[]{:S(2)}, u32[]{:S(2)}) collective-permute-start(f32[128,1024]{1,0:T(8,128)S(1)} %eval_jaxpr.50), channel_id=1, source_target_pairs={{0,1},{1,0},{2,3},{3,2},{4,5},{5,4},{6,7},{7,6},{8,9},{9,8},{10,11... | collective-permute-start | bytes 1572872 | tf_op jit(solution)/shard_map/while/body/eval_jaxpr/ppermute | solution.py:45
  283.7 12.3 %collective-permute-start.3 = (bf16[40,1024]{1,0:T(8,128)(2,1)S(1)}, bf16[40,1024]{1,0:T(8,128)(2,1)S(1)}, u32[]{:S(2)}, u32[]{:S(2)}) collective-permute-start(bf16[40,1024]{1,0:T(8,128)(2,1)S(1)} %get-tuple-element.592), channel_id=1, source_target_pairs={{0,32},{1,33},{2,34},{3,35},{4,36},{5,37},{6,38},{7,39},{32,64},{3... | collective-permute-start | bytes 245768 | tf_op jit(solution)/shard_map/while/body/eval_jaxpr/ppermute | solution.py:55
  296.1 16.9 %collective-permute-start.10 = (bf16[128,1024]{1,0:T(8,128)(2,1)S(1)}, bf16[128,1024]{1,0:T(8,128)(2,1)S(1)}, u32[]{:S(2)}, u32[]{:S(2)}) collective-permute-start(bf16[128,1024]{1,0:T(8,128)(2,1)S(1)} %get-tuple-element.627.stream), channel_id=1, source_target_pairs={{0,32},{32,64},{64,96},{96,128},{128,160},{160,192},{192,224},{224... | collective-permute-start | bytes 786440 | tf_op jit(solution)/shard_map/while/body/eval_jaxpr/ppermute | solution.py:40
  296.3 14.5 %collective-permute-start.7 = (bf16[80,1024]{1,0:T(8,128)(2,1)S(1)}, bf16[80,1024]{1,0:T(8,128)(2,1)S(1)}, u32[]{:S(2)}, u32[]{:S(2)}) collective-permute-start(bf16[80,1024]{1,0:T(8,128)(2,1)S(1)} %constant_dynamic-update-slice_fusion.15.refs_5_), channel_id=1, source_target_pairs={{0,24},{8,0},{16,8},{24,16},{1,25},{9,1},{17,9},{25,17},{2,26},{10... | collective-permute-start | bytes 491528 | tf_op jit(solution)/shard_map/while/body/eval_jaxpr/ppermute | solution.py:40
  357.0 15.3 %collective-permute-start.10 = (bf16[128,1024]{1,0:T(8,128)(2,1)S(1)}, bf16[128,1024]{1,0:T(8,128)(2,1)S(1)}, u32[]{:S(2)}, u32[]{:S(2)}) collective-permute-start(bf16[128,1024]{1,0:T(8,128)(2,1)S(1)} %get-tuple-element.627.stream), channel_id=1, source_target_pairs={{0,32},{32,64},{64,96},{96,128},{128,160},{160,192},{192,224},{224... | collective-permute-start | bytes 786440 | tf_op jit(solution)/shard_map/while/body/eval_jaxpr/ppermute | solution.py:40
  421.4 12.9 %collective-permute-start.10 = (bf16[128,1024]{1,0:T(8,128)(2,1)S(1)}, bf16[128,1024]{1,0:T(8,128)(2,1)S(1)}, u32[]{:S(2)}, u32[]{:S(2)}) collective-permute-start(bf16[128,1024]{1,0:T(8,128)(2,1)S(1)} %get-tuple-element.627.stream), channel_id=1, source_target_pairs={{0,32},{32,64},{64,96},{96,128},{128,160},{160,192},{192,224},{224... | collective-permute-start | bytes 786440 | tf_op jit(solution)/shard_map/while/body/eval_jaxpr/ppermute | solution.py:40
  466.5 13.5 %collective-permute-start.3 = (bf16[40,1024]{1,0:T(8,128)(2,1)S(1)}, bf16[40,1024]{1,0:T(8,128)(2,1)S(1)}, u32[]{:S(2)}, u32[]{:S(2)}) collective-permute-start(bf16[40,1024]{1,0:T(8,128)(2,1)S(1)} %get-tuple-element.592), channel_id=1, source_target_pairs={{0,32},{1,33},{2,34},{3,35},{4,36},{5,37},{6,38},{7,39},{32,64},{3... | collective-permute-start | bytes 245768 | tf_op jit(solution)/shard_map/while/body/eval_jaxpr/ppermute | solution.py:55
  480.2 16.2 %collective-permute-start.10 = (bf16[128,1024]{1,0:T(8,128)(2,1)S(1)}, bf16[128,1024]{1,0:T(8,128)(2,1)S(1)}, u32[]{:S(2)}, u32[]{:S(2)}) collective-permute-start(bf16[128,1024]{1,0:T(8,128)(2,1)S(1)} %get-tuple-element.627.stream), channel_id=1, source_target_pairs={{0,32},{32,64},{64,96},{96,128},{128,160},{160,192},{192,224},{224... | collective-permute-start | bytes 786440 | tf_op jit(solution)/shard_map/while/body/eval_jaxpr/ppermute | solution.py:40
  480.8 13.2 %collective-permute-start.7 = (bf16[80,1024]{1,0:T(8,128)(2,1)S(1)}, bf16[80,1024]{1,0:T(8,128)(2,1)S(1)}, u32[]{:S(2)}, u32[]{:S(2)}) collective-permute-start(bf16[80,1024]{1,0:T(8,128)(2,1)S(1)} %constant_dynamic-update-slice_fusion.15.refs_5_), channel_id=1, source_target_pairs={{0,24},{8,0},{16,8},{24,16},{1,25},{9,1},{17,9},{25,17},{2,26},{10... | collective-permute-start | bytes 491528 | tf_op jit(solution)/shard_map/while/body/eval_jaxpr/ppermute | solution.py:40
  517.0 11.9 %collective-permute-start.17 = (f32[128,1024]{1,0:T(8,128)S(1)}, f32[128,1024]{1,0:T(8,128)S(1)}, u32[]{:S(2)}, u32[]{:S(2)}) collective-permute-start(f32[128,1024]{1,0:T(8,128)S(1)} %eval_jaxpr.50), channel_id=1, source_target_pairs={{0,1},{1,0},{2,3},{3,2},{4,5},{5,4},{6,7},{7,6},{8,9},{9,8},{10,11... | collective-permute-start | bytes 1572872 | tf_op jit(solution)/shard_map/while/body/eval_jaxpr/ppermute | solution.py:45
  530.0 12.6 %collective-permute-start.1 = (bf16[40,1024]{1,0:T(8,128)(2,1)S(1)}, bf16[40,1024]{1,0:T(8,128)(2,1)S(1)}, u32[]{:S(2)}, u32[]{:S(2)}) collective-permute-start(bf16[40,1024]{1,0:T(8,128)(2,1)S(1)} %get-tuple-element.590), channel_id=1, source_target_pairs={{0,34},{1,35},{2,36},{3,37},{4,38},{5,39},{6,32},{7,33},{32,66},{3... | collective-permute-start | bytes 245768 | tf_op jit(solution)/shard_map/while/body/eval_jaxpr/ppermute | solution.py:55
  542.7 15.9 %collective-permute-start.10 = (bf16[128,1024]{1,0:T(8,128)(2,1)S(1)}, bf16[128,1024]{1,0:T(8,128)(2,1)S(1)}, u32[]{:S(2)}, u32[]{:S(2)}) collective-permute-start(bf16[128,1024]{1,0:T(8,128)(2,1)S(1)} %get-tuple-element.627.stream), channel_id=1, source_target_pairs={{0,32},{32,64},{64,96},{96,128},{128,160},{160,192},{192,224},{224... | collective-permute-start | bytes 786440 | tf_op jit(solution)/shard_map/while/body/eval_jaxpr/ppermute | solution.py:40
  (145 other events, 1125.0 us)

commit v3 on v2

--- a/solution.py
+++ b/solution.py
@@ -110,10 +110,12 @@
 
 
 def combine_kernel(which, high, low, *refs):
-    *blocks, out = refs
+    *blocks, out, swapped = refs
     rows = jnp.concatenate([block[...].astype(f32) for block in blocks]).astype(bf16)
     update = jnp.dot(high[which[0]], rows, preferred_element_type=f32)
-    out[...] = update + jnp.dot(low[which[0]], rows, preferred_element_type=f32)
+    update = update + jnp.dot(low[which[0]], rows, preferred_element_type=f32)
+    out[...] = update
+    swapped[...] = update.astype(bf16)
 
 
 def joined(halves, i):
@@ -142,7 +144,7 @@
     now = [pair(k, i, gate_buf, up_buf, sems) for i, k in enumerate(early)]
     later = [copy for i, k in enumerate(late) for copy in pair(k, i, gate_late, up_late, late_sems)]
     later += [pltpu.make_async_copy(w_down[i], down_out.at[i], down_sems.at[i]) for i in range(downs)]
-    for copy in [*now[0], *now[1], *later]:
+    for copy in [copy for pieces in now for copy in pieces] + later:
         copy.start()
     gate, up, squares = 0.0, 0.0, 0.0
     for i, k in enumerate(early):
@@ -238,23 +240,33 @@
 
     dispatch = kernel_call(dispatch_kernel, (SMEM, VMEM, VMEM), (shape(per_chip, width),) * chips, 8, flops=10**9)
     combine = kernel_call(
-        combine_kernel, (SMEM, VMEM, VMEM) + (VMEM,) * chips, shape(2 * local_tokens, width, kind=f32), 8, flops=10**9
-    )
-    early, late = (0, 1), (3, 2)
+        combine_kernel,
+        (SMEM, VMEM, VMEM) + (VMEM,) * chips,
+        (shape(2 * local_tokens, width, kind=f32), shape(2 * local_tokens, width)),
+        8,
+        flops=10**9,
+    )
+    early, late = (0,), (1, 3, 2)
+    order = (0, 1, 3, 2)
     gate_up_a = kernel_call(
         functools.partial(gate_up_first, early, late),
-        (SMEM, VMEM, HBM, HBM) + (HBM,) * ranks + (VMEM,) * 4,
+        (SMEM, VMEM, HBM, HBM) + (HBM,) * ranks + (VMEM,) * 2,
         (shape(rows, hidden_width, kind=f32),) * 2
         + (shape(rows, 128, kind=f32),)
-        + (shape(2, width, hidden_width),) * 2
+        + (shape(len(late), width, hidden_width),) * 2
         + (shape(ranks, hidden_width, width),),
         24,
-        [pltpu.VMEM((2, width, hidden_width), bf16)] * 2
-        + [pltpu.SemaphoreType.DMA((2, 2)), pltpu.SemaphoreType.DMA((2, 2)), pltpu.SemaphoreType.DMA((ranks,))],
+        [pltpu.VMEM((len(early), width, hidden_width), bf16)] * 2
+        + [pltpu.SemaphoreType.DMA((len(part), 2)) for part in (early, late)]
+        + [pltpu.SemaphoreType.DMA((ranks,))],
         flops=3 * 10**9,
     )
     gate_up_b = kernel_call(
-        functools.partial(gate_up_last, late, model_width), (VMEM,) * 10, shape(rows, hidden_width), 16, flops=10**9
+        functools.partial(gate_up_last, late, model_width),
+        (VMEM,) * (6 + 2 * len(late)),
+        shape(rows, hidden_width),
+        16,
+        flops=10**9,
     )
     down_a = kernel_call(down_first, (VMEM,) * 3, shape(rows, width, kind=f32), 16, flops=5 * 10**8)
     down_b = kernel_call(down_last, (VMEM,) * 4, (shape(per_chip, width),) * chips, 16, flops=5 * 10**8)
@@ -268,7 +280,7 @@
         halves = [jnp.concatenate([blocks[k] for k in pair]) for pair in BLOCK_PAIRS]
         slices = {k: [shifted(half, "tensor", k) for half in halves] for k in RANK_SHIFTS}
         slices[0] = halves
-        weights = [in_hbm(value) for value in (gate_matrix, up_matrix, *(down_parts[k] for k in (*early, *late)))]
+        weights = [in_hbm(value) for value in (gate_matrix, up_matrix, *(down_parts[k] for k in order))]
         gate, up, squares, gate_late, up_late, matrices = gate_up_a(
             rank_word, gain_parts, *weights, *(half for k in early for half in slices[k])
         )
@@ -276,10 +288,10 @@
         hidden, also = lax.optimization_barrier((hidden, also))
         hiddens = {k: shifted(hidden, "tensor", k) for k in RANK_SHIFTS}
         hiddens[0] = hidden
-        total = down_a(matrices, *(hiddens[k] for k in early))
-        outs = down_b(matrices, total, *(hiddens[k] for k in late))
-        order = [k for pair in BLOCK_PAIRS for k in pair]
-        return [outs[order.index(k)] for k in range(chips)], also
+        total = down_a(matrices, *(hiddens[k] for k in order[:2]))
+        outs = down_b(matrices, total, *(hiddens[k] for k in order[2:]))
+        blocks_out = [k for pair in BLOCK_PAIRS for k in pair]
+        return [outs[blocks_out.index(k)] for k in range(chips)], also
 
     def to_home(blocks):
         back = {k: shifted(blocks[k], "expert", groups - 2 * k) for k in CHIP_SHIFTS}
@@ -287,8 +299,8 @@
         return [back[k] for k in range(chips)]
 
     def combined(stream, blocks, which):
-        update = combine(which.reshape(1), high, low, *blocks)
-        return (stream.astype(f32) + (update + core_swap(update))).astype(bf16)
+        update, swapped = combine(which.reshape(1), high, low, *blocks)
+        return (stream.astype(f32) + (update + core_swap(swapped).astype(f32))).astype(bf16)
 
     def kept(collected, fresh, spot):
         own = lax.dynamic_slice_in_dim(fresh, core * local_tokens, local_tokens)[None]
@@ -316,7 +328,6 @@
         moved = {k: onward(outgoing[k], k) for k in (*CHIP_SHIFTS, 0)}
         stream = shifted(fresh, "pipe", 1)
         gains_here = marker(index.reshape(1), gain_parts)
-        gains_here = marker(index.reshape(1), gains_here)
         blocks, stream = expert_work([moved[k] for k in range(chips)], down_parts, stream, gains_here)
         fresh = combined(stream, to_home(blocks), jnp.clip(unit, 0, micro_count - 1))
         return fresh, kept(collected, fresh, jnp.clip(unit, 0, micro_count))

time: 590 us -> 625 us (1.059)
  waiting for transfers between devices: 214 us -> 284 us
  starting transfers between devices: 302 us -> 267 us
    ppermute x32, waiting for transfers between devices: 42.3 us -> 99.1 us  [onward(): return lax.ppermute(block, ('pipe', 'expert'), route)]
    ppermute x123, starting transfers between devices: 171 us -> 140 us  [shifted(): lax.ppermute(block, axis, [(i, (i + distance) % size) for i in range(size)])]
    ppermute x32, starting transfers between devices: 70.2 us -> 52.7 us  [onward(): return lax.ppermute(block, ('pipe', 'expert'), route)]
    ppermute x123, waiting for transfers between devices: 159 us -> 176 us  [shifted(): lax.ppermute(block, axis, [(i, (i + distance) % size) for i in range(size)])]
    ppermute x11, starting transfers between devices: 60.4 us -> 73.8 us  [core_swap(): return lax.ppermute(block, 'expert', [(i, i ^ 1) for i in range(size)])]
  transfers between devices with their start and end apart: 166 -> 166, of which waited for: 93 -> 105; matrix products, arithmetic and copies ran while one was open for 1% -> 1% of each run, Pallas kernels for 9% -> 8%
where the time goes in v3:
time: 625 us
  waiting for transfers between devices  284 us (45%)
  starting transfers between devices  267 us (43%)
  Pallas kernels  62.6 us (10%)
    ppermute x123, waiting for transfers between devices, shifted(): lax.ppermute(block, axis, [(i, (i + distance) % size) for i in range(size)])  176 us
    ppermute x123, starting transfers between devices, shifted(): lax.ppermute(block, axis, [(i, (i + distance) % size) for i in range(size)])  140 us
    ppermute x32, waiting for transfers between devices, onward(): return lax.ppermute(block, ('pipe', 'expert'), route)  99.1 us
    ppermute x11, starting transfers between devices, core_swap(): return lax.ppermute(block, 'expert', [(i, i ^ 1) for i in range(size)])  73.8 us
    ppermute x32, starting transfers between devices, onward(): return lax.ppermute(block, ('pipe', 'expert'), route)  52.7 us
    pallas_call x9, Pallas kernels, expert_work(): gate_up_a(rank_word, gain_parts, *weights, *(half for k in early for half...  34.8 us
  transfers between devices with their start and end apart: 166, of which 105 were waited for; matrix products, arithmetic and copies ran while one was open for 1% of the time, Pallas kernels for 8%

profile of v3, /device:TPU:1, one launch (start us, length us, event | category | flops | bytes accessed | tf_op | source)
XLA Modules:
  0.0 624.7 jit_solution(2654018035705080642)
XLA Ops:
  15.1 7.0 %collective-permute-start.23 = (bf16[40,1024]{1,0:T(8,128)(2,1)S(1)}, bf16[40,1024]{1,0:T(8,128)(2,1)S(1)}, u32[]{:S(2)}, u32[]{:S(2)}) collective-permute-start(bf16[40,1024]{1,0:T(8,128)(2,1)S(1)} %get-tuple-element.406), channel_id=1, source_target_pairs={{0,4},{1,5},{2,6},{3,7},{4,0},{5,1},{6,2},{7,3},{8,12},{9,13},{10,... | collective-permute-start | bytes 245768 | tf_op jit(solution)/shard_map/ppermute | solution.py:40
  31.5 19.2 %collective-permute-done.26.refs_0_ = bf16[80,1024]{1,0:T(8,128)(2,1)S(1)} collective-permute-done((bf16[80,1024]{1,0:T(8,128)(2,1)S(1)}, bf16[80,1024]{1,0:T(8,128)(2,1)S(1)}, u32[]{:S(2)}, u32[]{:S(2)}) %collective-permute-start.26) | collective-permute-done | bytes 163872 | tf_op jit(solution)/shard_map/ppermute | solution.py:40
  98.6 525.4 %while.17 = (s32[]{:T(128)}, bf16[128,1024]{1,0:T(8,128)(2,1)S(1)}, bf16[2,64,1024]{2,1,0:T(8,128)(2,1)S(1)}, f32[4,1024]{1,0:T(4,128)S(1)}, s32[]{:T(128)}, /*i...) while((s32[]{:T(128)}, bf16[128,1024]{1,0:T(8,128)(2,1)S(1)}, ...), condition=%wide.region_1.2_spmd, body=%wide.region_0.1_spmd.sunk | while | flops 7001720320 | bytes 12157964 | solution.py:335
  106.7 11.4 %collective-permute-done.3 = bf16[40,1024]{1,0:T(8,128)(2,1)S(1)} collective-permute-done((bf16[40,1024]{1,0:T(8,128)(2,1)S(1)}, bf16[40,1024]{1,0:T(8,128)(2,1)S(1)}, u32[]{:S(2)}, u32[]{:S(2)}) %collective-permute-start.3) | collective-permute-done | bytes 81952 | tf_op jit(solution)/shard_map/while/body/eval_jaxpr/ppermute | solution.py:55
  154.1 8.2 %collective-permute-start.17 = (bf16[128,1024]{1,0:T(8,128)(2,1)S(1)}, bf16[128,1024]{1,0:T(8,128)(2,1)S(1)}, u32[]{:S(2)}, u32[]{:S(2)}) collective-permute-start(bf16[128,1024]{1,0:T(8,128)(2,1)S(1)} %get-tuple-element.613), channel_id=1, source_target_pairs={{0,1},{1,0},{2,3},{3,2},{4,5},{5,4},{6,7},{7,6},{8,9},{9,8},{10,11... | collective-permute-start | bytes 786440 | tf_op jit(solution)/shard_map/while/body/eval_jaxpr/ppermute | solution.py:45
  164.8 5.1 collective-permute-start
  171.6 12.9 %collective-permute-done.3 = bf16[40,1024]{1,0:T(8,128)(2,1)S(1)} collective-permute-done((bf16[40,1024]{1,0:T(8,128)(2,1)S(1)}, bf16[40,1024]{1,0:T(8,128)(2,1)S(1)}, u32[]{:S(2)}, u32[]{:S(2)}) %collective-permute-start.3) | collective-permute-done | bytes 81952 | tf_op jit(solution)/shard_map/while/body/eval_jaxpr/ppermute | solution.py:55
  220.6 7.4 %collective-permute-start.17 = (bf16[128,1024]{1,0:T(8,128)(2,1)S(1)}, bf16[128,1024]{1,0:T(8,128)(2,1)S(1)}, u32[]{:S(2)}, u32[]{:S(2)}) collective-permute-start(bf16[128,1024]{1,0:T(8,128)(2,1)S(1)} %get-tuple-element.613), channel_id=1, source_target_pairs={{0,1},{1,0},{2,3},{3,2},{4,5},{5,4},{6,7},{7,6},{8,9},{9,8},{10,11... | collective-permute-start | bytes 786440 | tf_op jit(solution)/shard_map/while/body/eval_jaxpr/ppermute | solution.py:45
  237.2 12.6 %collective-permute-done.3 = bf16[40,1024]{1,0:T(8,128)(2,1)S(1)} collective-permute-done((bf16[40,1024]{1,0:T(8,128)(2,1)S(1)}, bf16[40,1024]{1,0:T(8,128)(2,1)S(1)}, u32[]{:S(2)}, u32[]{:S(2)}) %collective-permute-start.3) | collective-permute-done | bytes 81952 | tf_op jit(solution)/shard_map/while/body/eval_jaxpr/ppermute | solution.py:55
  285.8 8.6 %collective-permute-start.17 = (bf16[128,1024]{1,0:T(8,128)(2,1)S(1)}, bf16[128,1024]{1,0:T(8,128)(2,1)S(1)}, u32[]{:S(2)}, u32[]{:S(2)}) collective-permute-start(bf16[128,1024]{1,0:T(8,128)(2,1)S(1)} %get-tuple-element.613), channel_id=1, source_target_pairs={{0,1},{1,0},{2,3},{3,2},{4,5},{5,4},{6,7},{7,6},{8,9},{9,8},{10,11... | collective-permute-start | bytes 786440 | tf_op jit(solution)/shard_map/while/body/eval_jaxpr/ppermute | solution.py:45
  303.6 11.1 %collective-permute-done.3 = bf16[40,1024]{1,0:T(8,128)(2,1)S(1)} collective-permute-done((bf16[40,1024]{1,0:T(8,128)(2,1)S(1)}, bf16[40,1024]{1,0:T(8,128)(2,1)S(1)}, u32[]{:S(2)}, u32[]{:S(2)}) %collective-permute-start.3) | collective-permute-done | bytes 81952 | tf_op jit(solution)/shard_map/while/body/eval_jaxpr/ppermute | solution.py:55
  346.0 5.1 collective-permute-done.15.refs_2_
  351.4 8.5 %collective-permute-start.17 = (bf16[128,1024]{1,0:T(8,128)(2,1)S(1)}, bf16[128,1024]{1,0:T(8,128)(2,1)S(1)}, u32[]{:S(2)}, u32[]{:S(2)}) collective-permute-start(bf16[128,1024]{1,0:T(8,128)(2,1)S(1)} %get-tuple-element.613), channel_id=1, source_target_pairs={{0,1},{1,0},{2,3},{3,2},{4,5},{5,4},{6,7},{7,6},{8,9},{9,8},{10,11... | collective-permute-start | bytes 786440 | tf_op jit(solution)/shard_map/while/body/eval_jaxpr/ppermute | solution.py:45
  369.2 11.1 %collective-permute-done.3 = bf16[40,1024]{1,0:T(8,128)(2,1)S(1)} collective-permute-done((bf16[40,1024]{1,0:T(8,128)(2,1)S(1)}, bf16[40,1024]{1,0:T(8,128)(2,1)S(1)}, u32[]{:S(2)}, u32[]{:S(2)}) %collective-permute-start.3) | collective-permute-done | bytes 81952 | tf_op jit(solution)/shard_map/while/body/eval_jaxpr/ppermute | solution.py:55
  411.5 5.2 collective-permute-done.15.refs_2_
  417.0 8.7 %collective-permute-start.17 = (bf16[128,1024]{1,0:T(8,128)(2,1)S(1)}, bf16[128,1024]{1,0:T(8,128)(2,1)S(1)}, u32[]{:S(2)}, u32[]{:S(2)}) collective-permute-start(bf16[128,1024]{1,0:T(8,128)(2,1)S(1)} %get-tuple-element.613), channel_id=1, source_target_pairs={{0,1},{1,0},{2,3},{3,2},{4,5},{5,4},{6,7},{7,6},{8,9},{9,8},{10,11... | collective-permute-start | bytes 786440 | tf_op jit(solution)/shard_map/while/body/eval_jaxpr/ppermute | solution.py:45
  435.0 11.1 %collective-permute-done.3 = bf16[40,1024]{1,0:T(8,128)(2,1)S(1)} collective-permute-done((bf16[40,1024]{1,0:T(8,128)(2,1)S(1)}, bf16[40,1024]{1,0:T(8,128)(2,1)S(1)}, u32[]{:S(2)}, u32[]{:S(2)}) %collective-permute-start.3) | collective-permute-done | bytes 81952 | tf_op jit(solution)/shard_map/while/body/eval_jaxpr/ppermute | solution.py:55
  477.3 5.4 collective-permute-done.15.refs_2_
  482.9 8.5 %collective-permute-start.17 = (bf16[128,1024]{1,0:T(8,128)(2,1)S(1)}, bf16[128,1024]{1,0:T(8,128)(2,1)S(1)}, u32[]{:S(2)}, u32[]{:S(2)}) collective-permute-start(bf16[128,1024]{1,0:T(8,128)(2,1)S(1)} %get-tuple-element.613), channel_id=1, source_target_pairs={{0,1},{1,0},{2,3},{3,2},{4,5},{5,4},{6,7},{7,6},{8,9},{9,8},{10,11... | collective-permute-start | bytes 786440 | tf_op jit(solution)/shard_map/while/body/eval_jaxpr/ppermute | solution.py:45
  500.6 11.2 %collective-permute-done.3 = bf16[40,1024]{1,0:T(8,128)(2,1)S(1)} collective-permute-done((bf16[40,1024]{1,0:T(8,128)(2,1)S(1)}, bf16[40,1024]{1,0:T(8,128)(2,1)S(1)}, u32[]{:S(2)}, u32[]{:S(2)}) %collective-permute-start.3) | collective-permute-done | bytes 81952 | tf_op jit(solution)/shard_map/while/body/eval_jaxpr/ppermute | solution.py:55
  542.8 6.1 collective-permute-done.15.refs_2_
  549.2 8.2 %collective-permute-start.17 = (bf16[128,1024]{1,0:T(8,128)(2,1)S(1)}, bf16[128,1024]{1,0:T(8,128)(2,1)S(1)}, u32[]{:S(2)}, u32[]{:S(2)}) collective-permute-start(bf16[128,1024]{1,0:T(8,128)(2,1)S(1)} %get-tuple-element.613), channel_id=1, source_target_pairs={{0,1},{1,0},{2,3},{3,2},{4,5},{5,4},{6,7},{7,6},{8,9},{9,8},{10,11... | collective-permute-start | bytes 786440 | tf_op jit(solution)/shard_map/while/body/eval_jaxpr/ppermute | solution.py:45
  567.7 10.2 %collective-permute-done.3 = bf16[40,1024]{1,0:T(8,128)(2,1)S(1)} collective-permute-done((bf16[40,1024]{1,0:T(8,128)(2,1)S(1)}, bf16[40,1024]{1,0:T(8,128)(2,1)S(1)}, u32[]{:S(2)}, u32[]{:S(2)}) %collective-permute-start.3) | collective-permute-done | bytes 81952 | tf_op jit(solution)/shard_map/while/body/eval_jaxpr/ppermute | solution.py:55
  614.2 8.5 %collective-permute-start.17 = (bf16[128,1024]{1,0:T(8,128)(2,1)S(1)}, bf16[128,1024]{1,0:T(8,128)(2,1)S(1)}, u32[]{:S(2)}, u32[]{:S(2)}) collective-permute-start(bf16[128,1024]{1,0:T(8,128)(2,1)S(1)} %get-tuple-element.613), channel_id=1, source_target_pairs={{0,1},{1,0},{2,3},{3,2},{4,5},{5,4},{6,7},{7,6},{8,9},{9,8},{10,11... | collective-permute-start | bytes 786440 | tf_op jit(solution)/shard_map/while/body/eval_jaxpr/ppermute | solution.py:45
  (450 shorter events, 411.9 us)
Async XLA Ops:
  9.7 41.5 %collective-permute-start.19 = (bf16[384,1024]{1,0:T(8,128)(2,1)}, bf16[384,1024]{1,0:T(8,128)(2,1)S(1)}, u32[]{:S(2)}, u32[]{:S(2)}) collective-permute-start(bf16[384,1024]{1,0:T(8,128)(2,1)} %get-tuple-element.465), channel_id=1, source_target_pairs={{0,8},{8,16},{16,24},{24,0},{1,9},{9,17},{17,25},{25,1},{2,10},{10... | collective-permute-start | bytes 2359304 | tf_op jit(solution)/shard_map/ppermute | solution.py:40
  9.7 41.6 %collective-permute-start.20 = (bf16[384,1024]{1,0:T(8,128)(2,1)}, bf16[384,1024]{1,0:T(8,128)(2,1)}, u32[]{:S(2)}, u32[]{:S(2)}) collective-permute-start(bf16[384,1024]{1,0:T(8,128)(2,1)} %get-tuple-element.467), channel_id=1, source_target_pairs={{0,24},{8,0},{16,8},{24,16},{1,25},{9,1},{17,9},{25,17},{2,26},{10... | collective-permute-start | bytes 2359304 | tf_op jit(solution)/shard_map/ppermute | solution.py:40
  12.5 41.5 %collective-permute-start.21 = (bf16[384,1024]{1,0:T(8,128)(2,1)S(1)}, bf16[384,1024]{1,0:T(8,128)(2,1)S(1)}, u32[]{:S(2)}, u32[]{:S(2)}) collective-permute-start(bf16[384,1024]{1,0:T(8,128)(2,1)S(1)} %get-tuple-element.464), channel_id=1, source_target_pairs={{0,16},{8,24},{16,0},{24,8},{1,17},{9,25},{17,1},{25,9},{2,18},{10... | collective-permute-start | bytes 2359304 | tf_op jit(solution)/shard_map/ppermute | solution.py:40
  28.6 22.1 %collective-permute-start.26 = (bf16[80,1024]{1,0:T(8,128)(2,1)S(1)}, bf16[80,1024]{1,0:T(8,128)(2,1)S(1)}, u32[]{:S(2)}, u32[]{:S(2)}) collective-permute-start(bf16[80,1024]{1,0:T(8,128)(2,1)S(1)} %constant_dynamic-update-slice_fusion.4.refs_4_), channel_id=1, source_target_pairs={{0,8},{8,16},{16,24},{24,0},{1,9},{9,17},{17,25},{25,1},{2,10},{10... | collective-permute-start | bytes 491528 | tf_op jit(solution)/shard_map/ppermute | solution.py:40
  30.1 28.9 %collective-permute-start.28 = (bf16[80,1024]{1,0:T(8,128)(2,1)S(1)}, bf16[80,1024]{1,0:T(8,128)(2,1)S(1)}, u32[]{:S(2)}, u32[]{:S(2)}) collective-permute-start(bf16[80,1024]{1,0:T(8,128)(2,1)S(1)} %constant_dynamic-update-slice_fusion.4.refs_4_), channel_id=1, source_target_pairs={{0,24},{8,0},{16,8},{24,16},{1,25},{9,1},{17,9},{25,17},{2,26},{10... | collective-permute-start | bytes 491528 | tf_op jit(solution)/shard_map/ppermute | solution.py:40
  99.7 35.0 %collective-permute-start.10 = (bf16[128,1024]{1,0:T(8,128)(2,1)S(1)}, bf16[128,1024]{1,0:T(8,128)(2,1)S(1)}, u32[]{:S(2)}, u32[]{:S(2)}) collective-permute-start(bf16[128,1024]{1,0:T(8,128)(2,1)S(1)} %get-tuple-element.637.stream), channel_id=1, source_target_pairs={{0,32},{32,64},{64,96},{96,128},{128,160},{160,192},{192,224},{224... | collective-permute-start | bytes 786440 | tf_op jit(solution)/shard_map/while/body/eval_jaxpr/ppermute | solution.py:40
  102.1 18.8 %collective-permute-start = (bf16[40,1024]{1,0:T(8,128)(2,1)S(1)}, bf16[40,1024]{1,0:T(8,128)(2,1)S(1)}, u32[]{:S(2)}, u32[]{:S(2)}) collective-permute-start(bf16[40,1024]{1,0:T(8,128)(2,1)S(1)} %get-tuple-element.597), channel_id=1, source_target_pairs={{0,36},{1,37},{2,38},{3,39},{4,32},{5,33},{6,34},{7,35},{32,68},{3... | collective-permute-start | bytes 245768 | tf_op jit(solution)/shard_map/while/body/eval_jaxpr/ppermute | solution.py:55
  164.0 38.4 %collective-permute-start.10 = (bf16[128,1024]{1,0:T(8,128)(2,1)S(1)}, bf16[128,1024]{1,0:T(8,128)(2,1)S(1)}, u32[]{:S(2)}, u32[]{:S(2)}) collective-permute-start(bf16[128,1024]{1,0:T(8,128)(2,1)S(1)} %get-tuple-element.637.stream), channel_id=1, source_target_pairs={{0,32},{32,64},{64,96},{96,128},{128,160},{160,192},{192,224},{224... | collective-permute-start | bytes 786440 | tf_op jit(solution)/shard_map/while/body/eval_jaxpr/ppermute | solution.py:40
  164.1 20.3 %collective-permute-start.3 = (bf16[40,1024]{1,0:T(8,128)(2,1)S(1)}, bf16[40,1024]{1,0:T(8,128)(2,1)S(1)}, u32[]{:S(2)}, u32[]{:S(2)}) collective-permute-start(bf16[40,1024]{1,0:T(8,128)(2,1)S(1)} %get-tuple-element.600), channel_id=1, source_target_pairs={{0,32},{1,33},{2,34},{3,35},{4,36},{5,37},{6,38},{7,39},{32,64},{3... | collective-permute-start | bytes 245768 | tf_op jit(solution)/shard_map/while/body/eval_jaxpr/ppermute | solution.py:55
  164.8 22.3 %collective-permute-start = (bf16[40,1024]{1,0:T(8,128)(2,1)S(1)}, bf16[40,1024]{1,0:T(8,128)(2,1)S(1)}, u32[]{:S(2)}, u32[]{:S(2)}) collective-permute-start(bf16[40,1024]{1,0:T(8,128)(2,1)S(1)} %get-tuple-element.597), channel_id=1, source_target_pairs={{0,36},{1,37},{2,38},{3,39},{4,32},{5,33},{6,34},{7,35},{32,68},{3... | collective-permute-start | bytes 245768 | tf_op jit(solution)/shard_map/while/body/eval_jaxpr/ppermute | solution.py:55
  229.7 37.8 %collective-permute-start.10 = (bf16[128,1024]{1,0:T(8,128)(2,1)S(1)}, bf16[128,1024]{1,0:T(8,128)(2,1)S(1)}, u32[]{:S(2)}, u32[]{:S(2)}) collective-permute-start(bf16[128,1024]{1,0:T(8,128)(2,1)S(1)} %get-tuple-element.637.stream), channel_id=1, source_target_pairs={{0,32},{32,64},{64,96},{96,128},{128,160},{160,192},{192,224},{224... | collective-permute-start | bytes 786440 | tf_op jit(solution)/shard_map/while/body/eval_jaxpr/ppermute | solution.py:40
  229.8 20.0 %collective-permute-start.3 = (bf16[40,1024]{1,0:T(8,128)(2,1)S(1)}, bf16[40,1024]{1,0:T(8,128)(2,1)S(1)}, u32[]{:S(2)}, u32[]{:S(2)}) collective-permute-start(bf16[40,1024]{1,0:T(8,128)(2,1)S(1)} %get-tuple-element.600), channel_id=1, source_target_pairs={{0,32},{1,33},{2,34},{3,35},{4,36},{5,37},{6,38},{7,39},{32,64},{3... | collective-permute-start | bytes 245768 | tf_op jit(solution)/shard_map/while/body/eval_jaxpr/ppermute | solution.py:55
  230.1 22.3 %collective-permute-start = (bf16[40,1024]{1,0:T(8,128)(2,1)S(1)}, bf16[40,1024]{1,0:T(8,128)(2,1)S(1)}, u32[]{:S(2)}, u32[]{:S(2)}) collective-permute-start(bf16[40,1024]{1,0:T(8,128)(2,1)S(1)} %get-tuple-element.597), channel_id=1, source_target_pairs={{0,36},{1,37},{2,38},{3,39},{4,32},{5,33},{6,34},{7,35},{32,68},{3... | collective-permute-start | bytes 245768 | tf_op jit(solution)/shard_map/while/body/eval_jaxpr/ppermute | solution.py:55
  296.1 36.0 %collective-permute-start.10 = (bf16[128,1024]{1,0:T(8,128)(2,1)S(1)}, bf16[128,1024]{1,0:T(8,128)(2,1)S(1)}, u32[]{:S(2)}, u32[]{:S(2)}) collective-permute-start(bf16[128,1024]{1,0:T(8,128)(2,1)S(1)} %get-tuple-element.637.stream), channel_id=1, source_target_pairs={{0,32},{32,64},{64,96},{96,128},{128,160},{160,192},{192,224},{224... | collective-permute-start | bytes 786440 | tf_op jit(solution)/shard_map/while/body/eval_jaxpr/ppermute | solution.py:40
  296.2 21.2 %collective-permute-start = (bf16[40,1024]{1,0:T(8,128)(2,1)S(1)}, bf16[40,1024]{1,0:T(8,128)(2,1)S(1)}, u32[]{:S(2)}, u32[]{:S(2)}) collective-permute-start(bf16[40,1024]{1,0:T(8,128)(2,1)S(1)} %get-tuple-element.597), channel_id=1, source_target_pairs={{0,36},{1,37},{2,38},{3,39},{4,32},{5,33},{6,34},{7,35},{32,68},{3... | collective-permute-start | bytes 245768 | tf_op jit(solution)/shard_map/while/body/eval_jaxpr/ppermute | solution.py:55
  361.7 36.0 %collective-permute-start.10 = (bf16[128,1024]{1,0:T(8,128)(2,1)S(1)}, bf16[128,1024]{1,0:T(8,128)(2,1)S(1)}, u32[]{:S(2)}, u32[]{:S(2)}) collective-permute-start(bf16[128,1024]{1,0:T(8,128)(2,1)S(1)} %get-tuple-element.637.stream), channel_id=1, source_target_pairs={{0,32},{32,64},{64,96},{96,128},{128,160},{160,192},{192,224},{224... | collective-permute-start | bytes 786440 | tf_op jit(solution)/shard_map/while/body/eval_jaxpr/ppermute | solution.py:40
  361.8 21.1 %collective-permute-start = (bf16[40,1024]{1,0:T(8,128)(2,1)S(1)}, bf16[40,1024]{1,0:T(8,128)(2,1)S(1)}, u32[]{:S(2)}, u32[]{:S(2)}) collective-permute-start(bf16[40,1024]{1,0:T(8,128)(2,1)S(1)} %get-tuple-element.597), channel_id=1, source_target_pairs={{0,36},{1,37},{2,38},{3,39},{4,32},{5,33},{6,34},{7,35},{32,68},{3... | collective-permute-start | bytes 245768 | tf_op jit(solution)/shard_map/while/body/eval_jaxpr/ppermute | solution.py:55
  427.4 35.9 %collective-permute-start.10 = (bf16[128,1024]{1,0:T(8,128)(2,1)S(1)}, bf16[128,1024]{1,0:T(8,128)(2,1)S(1)}, u32[]{:S(2)}, u32[]{:S(2)}) collective-permute-start(bf16[128,1024]{1,0:T(8,128)(2,1)S(1)} %get-tuple-element.637.stream), channel_id=1, source_target_pairs={{0,32},{32,64},{64,96},{96,128},{128,160},{160,192},{192,224},{224... | collective-permute-start | bytes 786440 | tf_op jit(solution)/shard_map/while/body/eval_jaxpr/ppermute | solution.py:40
  427.6 21.1 %collective-permute-start = (bf16[40,1024]{1,0:T(8,128)(2,1)S(1)}, bf16[40,1024]{1,0:T(8,128)(2,1)S(1)}, u32[]{:S(2)}, u32[]{:S(2)}) collective-permute-start(bf16[40,1024]{1,0:T(8,128)(2,1)S(1)} %get-tuple-element.597), channel_id=1, source_target_pairs={{0,36},{1,37},{2,38},{3,39},{4,32},{5,33},{6,34},{7,35},{32,68},{3... | collective-permute-start | bytes 245768 | tf_op jit(solution)/shard_map/while/body/eval_jaxpr/ppermute | solution.py:55
  493.1 36.0 %collective-permute-start.10 = (bf16[128,1024]{1,0:T(8,128)(2,1)S(1)}, bf16[128,1024]{1,0:T(8,128)(2,1)S(1)}, u32[]{:S(2)}, u32[]{:S(2)}) collective-permute-start(bf16[128,1024]{1,0:T(8,128)(2,1)S(1)} %get-tuple-element.637.stream), channel_id=1, source_target_pairs={{0,32},{32,64},{64,96},{96,128},{128,160},{160,192},{192,224},{224... | collective-permute-start | bytes 786440 | tf_op jit(solution)/shard_map/while/body/eval_jaxpr/ppermute | solution.py:40
  493.3 21.2 %collective-permute-start = (bf16[40,1024]{1,0:T(8,128)(2,1)S(1)}, bf16[40,1024]{1,0:T(8,128)(2,1)S(1)}, u32[]{:S(2)}, u32[]{:S(2)}) collective-permute-start(bf16[40,1024]{1,0:T(8,128)(2,1)S(1)} %get-tuple-element.597), channel_id=1, source_target_pairs={{0,36},{1,37},{2,38},{3,39},{4,32},{5,33},{6,34},{7,35},{32,68},{3... | collective-permute-start | bytes 245768 | tf_op jit(solution)/shard_map/while/body/eval_jaxpr/ppermute | solution.py:55
  559.1 36.1 %collective-permute-start.10 = (bf16[128,1024]{1,0:T(8,128)(2,1)S(1)}, bf16[128,1024]{1,0:T(8,128)(2,1)S(1)}, u32[]{:S(2)}, u32[]{:S(2)}) collective-permute-start(bf16[128,1024]{1,0:T(8,128)(2,1)S(1)} %get-tuple-element.637.stream), channel_id=1, source_target_pairs={{0,32},{32,64},{64,96},{96,128},{128,160},{160,192},{192,224},{224... | collective-permute-start | bytes 786440 | tf_op jit(solution)/shard_map/while/body/eval_jaxpr/ppermute | solution.py:40
  559.2 18.7 %collective-permute-start.3 = (bf16[40,1024]{1,0:T(8,128)(2,1)S(1)}, bf16[40,1024]{1,0:T(8,128)(2,1)S(1)}, u32[]{:S(2)}, u32[]{:S(2)}) collective-permute-start(bf16[40,1024]{1,0:T(8,128)(2,1)S(1)} %get-tuple-element.600), channel_id=1, source_target_pairs={{0,32},{1,33},{2,34},{3,35},{4,36},{5,37},{6,38},{7,39},{32,64},{3... | collective-permute-start | bytes 245768 | tf_op jit(solution)/shard_map/while/body/eval_jaxpr/ppermute | solution.py:55
  559.3 21.3 %collective-permute-start = (bf16[40,1024]{1,0:T(8,128)(2,1)S(1)}, bf16[40,1024]{1,0:T(8,128)(2,1)S(1)}, u32[]{:S(2)}, u32[]{:S(2)}) collective-permute-start(bf16[40,1024]{1,0:T(8,128)(2,1)S(1)} %get-tuple-element.597), channel_id=1, source_target_pairs={{0,36},{1,37},{2,38},{3,39},{4,32},{5,33},{6,34},{7,35},{32,68},{3... | collective-permute-start | bytes 245768 | tf_op jit(solution)/shard_map/while/body/eval_jaxpr/ppermute | solution.py:55
  (147 other events, 1211.8 us)

commit v4 on v3

--- a/solution.py
+++ b/solution.py
@@ -176,15 +176,15 @@
     hidden[...] = (gate / (1.0 + jnp.exp(-gate)) * (up * inv_rms)).astype(bf16)
 
 
-def down_first(matrices, own, guest, out):
-    out[...] = jnp.dot(own[...], matrices[0], preferred_element_type=f32) + jnp.dot(
-        guest[...], matrices[1], preferred_element_type=f32
-    )
-
-
-def down_last(matrices, before, one, other, *outs):
-    total = before[...] + jnp.dot(one[...], matrices[2], preferred_element_type=f32)
-    total = total + jnp.dot(other[...], matrices[3], preferred_element_type=f32)
+def down_first(matrices, own, out):
+    out[...] = jnp.dot(own[...], matrices[0], preferred_element_type=f32)
+
+
+def down_last(matrices, before, *refs):
+    parts, outs = refs[:3], refs[3:]
+    total = before[...]
+    for i, part in enumerate(parts, 1):
+        total = total + jnp.dot(part[...], matrices[i], preferred_element_type=f32)
     size = outs[0].shape[0]
     for k, piece in enumerate(outs):
         piece[...] = total[k * size : (k + 1) * size].astype(bf16)
@@ -268,8 +268,8 @@
         16,
         flops=10**9,
     )
-    down_a = kernel_call(down_first, (VMEM,) * 3, shape(rows, width, kind=f32), 16, flops=5 * 10**8)
-    down_b = kernel_call(down_last, (VMEM,) * 4, (shape(per_chip, width),) * chips, 16, flops=5 * 10**8)
+    down_a = kernel_call(down_first, (VMEM,) * 2, shape(rows, width, kind=f32), 16, flops=5 * 10**8)
+    down_b = kernel_call(down_last, (VMEM,) * 5, (shape(per_chip, width),) * chips, 16, flops=5 * 10**8)
 
     rank_word = rank.reshape(1).astype(i32)
     gain_parts = jnp.concatenate([slice_at(gains, rank - k, 1) for k in range(ranks)])
@@ -288,8 +288,8 @@
         hidden, also = lax.optimization_barrier((hidden, also))
         hiddens = {k: shifted(hidden, "tensor", k) for k in RANK_SHIFTS}
         hiddens[0] = hidden
-        total = down_a(matrices, *(hiddens[k] for k in order[:2]))
-        outs = down_b(matrices, total, *(hiddens[k] for k in order[2:]))
+        total = down_a(matrices, *(hiddens[k] for k in order[:1]))
+        outs = down_b(matrices, total, *(hiddens[k] for k in order[1:]))
         blocks_out = [k for pair in BLOCK_PAIRS for k in pair]
         return [outs[blocks_out.index(k)] for k in range(chips)], also
 

time: 625 us -> 626 us (level)
  no operation moved by 1% of the time
where the time goes in v4:
time: 626 us
  waiting for transfers between devices  285 us (46%)
  starting transfers between devices  267 us (43%)
  Pallas kernels  62.6 us (10%)
    ppermute x123, waiting for transfers between devices, shifted(): lax.ppermute(block, axis, [(i, (i + distance) % size) for i in range(size)])  177 us
    ppermute x123, starting transfers between devices, shifted(): lax.ppermute(block, axis, [(i, (i + distance) % size) for i in range(size)])  140 us
    ppermute x32, waiting for transfers between devices, onward(): return lax.ppermute(block, ('pipe', 'expert'), route)  99.1 us
    ppermute x11, starting transfers between devices, core_swap(): return lax.ppermute(block, 'expert', [(i, i ^ 1) for i in range(size)])  73.8 us
    ppermute x32, starting transfers between devices, onward(): return lax.ppermute(block, ('pipe', 'expert'), route)  52.7 us
    pallas_call x9, Pallas kernels, expert_work(): gate_up_a(rank_word, gain_parts, *weights, *(half for k in early for half...  34.8 us
  transfers between devices with their start and end apart: 166, of which 105 were waited for; matrix products, arithmetic and copies ran while one was open for 1% of the time, Pallas kernels for 8%

profile of v4, /device:TPU:1, one launch (start us, length us, event | category | flops | bytes accessed | tf_op | source)
XLA Modules:
  0.0 626.2 jit_solution(11784654830414824194)
XLA Ops:
  15.1 7.0 %collective-permute-start.23 = (bf16[40,1024]{1,0:T(8,128)(2,1)S(1)}, bf16[40,1024]{1,0:T(8,128)(2,1)S(1)}, u32[]{:S(2)}, u32[]{:S(2)}) collective-permute-start(bf16[40,1024]{1,0:T(8,128)(2,1)S(1)} %get-tuple-element.406), channel_id=1, source_target_pairs={{0,4},{1,5},{2,6},{3,7},{4,0},{5,1},{6,2},{7,3},{8,12},{9,13},{10,... | collective-permute-start | bytes 245768 | tf_op jit(solution)/shard_map/ppermute | solution.py:40
  31.5 19.2 %collective-permute-done.26.refs_0_ = bf16[80,1024]{1,0:T(8,128)(2,1)S(1)} collective-permute-done((bf16[80,1024]{1,0:T(8,128)(2,1)S(1)}, bf16[80,1024]{1,0:T(8,128)(2,1)S(1)}, u32[]{:S(2)}, u32[]{:S(2)}) %collective-permute-start.26) | collective-permute-done | bytes 163872 | tf_op jit(solution)/shard_map/ppermute | solution.py:40
  98.8 526.7 %while.17 = (s32[]{:T(128)}, bf16[128,1024]{1,0:T(8,128)(2,1)S(1)}, bf16[2,64,1024]{2,1,0:T(8,128)(2,1)S(1)}, f32[4,1024]{1,0:T(4,128)S(1)}, s32[]{:T(128)}, /*i...) while((s32[]{:T(128)}, bf16[128,1024]{1,0:T(8,128)(2,1)S(1)}, ...), condition=%wide.region_1.2_spmd, body=%wide.region_0.1_spmd.sunk | while | flops 7001720320 | bytes 12157964 | solution.py:335
  106.9 11.4 %collective-permute-done.3 = bf16[40,1024]{1,0:T(8,128)(2,1)S(1)} collective-permute-done((bf16[40,1024]{1,0:T(8,128)(2,1)S(1)}, bf16[40,1024]{1,0:T(8,128)(2,1)S(1)}, u32[]{:S(2)}, u32[]{:S(2)}) %collective-permute-start.3) | collective-permute-done | bytes 81952 | tf_op jit(solution)/shard_map/while/body/eval_jaxpr/ppermute | solution.py:55
  154.5 8.2 %collective-permute-start.17 = (bf16[128,1024]{1,0:T(8,128)(2,1)S(1)}, bf16[128,1024]{1,0:T(8,128)(2,1)S(1)}, u32[]{:S(2)}, u32[]{:S(2)}) collective-permute-start(bf16[128,1024]{1,0:T(8,128)(2,1)S(1)} %get-tuple-element.613), channel_id=1, source_target_pairs={{0,1},{1,0},{2,3},{3,2},{4,5},{5,4},{6,7},{7,6},{8,9},{9,8},{10,11... | collective-permute-start | bytes 786440 | tf_op jit(solution)/shard_map/while/body/eval_jaxpr/ppermute | solution.py:45
  165.1 5.1 collective-permute-start
  171.9 12.9 %collective-permute-done.3 = bf16[40,1024]{1,0:T(8,128)(2,1)S(1)} collective-permute-done((bf16[40,1024]{1,0:T(8,128)(2,1)S(1)}, bf16[40,1024]{1,0:T(8,128)(2,1)S(1)}, u32[]{:S(2)}, u32[]{:S(2)}) %collective-permute-start.3) | collective-permute-done | bytes 81952 | tf_op jit(solution)/shard_map/while/body/eval_jaxpr/ppermute | solution.py:55
  221.1 7.4 %collective-permute-start.17 = (bf16[128,1024]{1,0:T(8,128)(2,1)S(1)}, bf16[128,1024]{1,0:T(8,128)(2,1)S(1)}, u32[]{:S(2)}, u32[]{:S(2)}) collective-permute-start(bf16[128,1024]{1,0:T(8,128)(2,1)S(1)} %get-tuple-element.613), channel_id=1, source_target_pairs={{0,1},{1,0},{2,3},{3,2},{4,5},{5,4},{6,7},{7,6},{8,9},{9,8},{10,11... | collective-permute-start | bytes 786440 | tf_op jit(solution)/shard_map/while/body/eval_jaxpr/ppermute | solution.py:45
  237.7 12.6 %collective-permute-done.3 = bf16[40,1024]{1,0:T(8,128)(2,1)S(1)} collective-permute-done((bf16[40,1024]{1,0:T(8,128)(2,1)S(1)}, bf16[40,1024]{1,0:T(8,128)(2,1)S(1)}, u32[]{:S(2)}, u32[]{:S(2)}) %collective-permute-start.3) | collective-permute-done | bytes 81952 | tf_op jit(solution)/shard_map/while/body/eval_jaxpr/ppermute | solution.py:55
  286.4 8.6 %collective-permute-start.17 = (bf16[128,1024]{1,0:T(8,128)(2,1)S(1)}, bf16[128,1024]{1,0:T(8,128)(2,1)S(1)}, u32[]{:S(2)}, u32[]{:S(2)}) collective-permute-start(bf16[128,1024]{1,0:T(8,128)(2,1)S(1)} %get-tuple-element.613), channel_id=1, source_target_pairs={{0,1},{1,0},{2,3},{3,2},{4,5},{5,4},{6,7},{7,6},{8,9},{9,8},{10,11... | collective-permute-start | bytes 786440 | tf_op jit(solution)/shard_map/while/body/eval_jaxpr/ppermute | solution.py:45
  304.2 11.1 %collective-permute-done.3 = bf16[40,1024]{1,0:T(8,128)(2,1)S(1)} collective-permute-done((bf16[40,1024]{1,0:T(8,128)(2,1)S(1)}, bf16[40,1024]{1,0:T(8,128)(2,1)S(1)}, u32[]{:S(2)}, u32[]{:S(2)}) %collective-permute-start.3) | collective-permute-done | bytes 81952 | tf_op jit(solution)/shard_map/while/body/eval_jaxpr/ppermute | solution.py:55
  346.8 5.1 collective-permute-done.15.refs_2_
  352.3 8.5 %collective-permute-start.17 = (bf16[128,1024]{1,0:T(8,128)(2,1)S(1)}, bf16[128,1024]{1,0:T(8,128)(2,1)S(1)}, u32[]{:S(2)}, u32[]{:S(2)}) collective-permute-start(bf16[128,1024]{1,0:T(8,128)(2,1)S(1)} %get-tuple-element.613), channel_id=1, source_target_pairs={{0,1},{1,0},{2,3},{3,2},{4,5},{5,4},{6,7},{7,6},{8,9},{9,8},{10,11... | collective-permute-start | bytes 786440 | tf_op jit(solution)/shard_map/while/body/eval_jaxpr/ppermute | solution.py:45
  370.0 11.1 %collective-permute-done.3 = bf16[40,1024]{1,0:T(8,128)(2,1)S(1)} collective-permute-done((bf16[40,1024]{1,0:T(8,128)(2,1)S(1)}, bf16[40,1024]{1,0:T(8,128)(2,1)S(1)}, u32[]{:S(2)}, u32[]{:S(2)}) %collective-permute-start.3) | collective-permute-done | bytes 81952 | tf_op jit(solution)/shard_map/while/body/eval_jaxpr/ppermute | solution.py:55
  412.5 5.2 collective-permute-done.15.refs_2_
  418.0 8.7 %collective-permute-start.17 = (bf16[128,1024]{1,0:T(8,128)(2,1)S(1)}, bf16[128,1024]{1,0:T(8,128)(2,1)S(1)}, u32[]{:S(2)}, u32[]{:S(2)}) collective-permute-start(bf16[128,1024]{1,0:T(8,128)(2,1)S(1)} %get-tuple-element.613), channel_id=1, source_target_pairs={{0,1},{1,0},{2,3},{3,2},{4,5},{5,4},{6,7},{7,6},{8,9},{9,8},{10,11... | collective-permute-start | bytes 786440 | tf_op jit(solution)/shard_map/while/body/eval_jaxpr/ppermute | solution.py:45
  436.0 11.1 %collective-permute-done.3 = bf16[40,1024]{1,0:T(8,128)(2,1)S(1)} collective-permute-done((bf16[40,1024]{1,0:T(8,128)(2,1)S(1)}, bf16[40,1024]{1,0:T(8,128)(2,1)S(1)}, u32[]{:S(2)}, u32[]{:S(2)}) %collective-permute-start.3) | collective-permute-done | bytes 81952 | tf_op jit(solution)/shard_map/while/body/eval_jaxpr/ppermute | solution.py:55
  478.4 5.4 collective-permute-done.15.refs_2_
  484.1 8.5 %collective-permute-start.17 = (bf16[128,1024]{1,0:T(8,128)(2,1)S(1)}, bf16[128,1024]{1,0:T(8,128)(2,1)S(1)}, u32[]{:S(2)}, u32[]{:S(2)}) collective-permute-start(bf16[128,1024]{1,0:T(8,128)(2,1)S(1)} %get-tuple-element.613), channel_id=1, source_target_pairs={{0,1},{1,0},{2,3},{3,2},{4,5},{5,4},{6,7},{7,6},{8,9},{9,8},{10,11... | collective-permute-start | bytes 786440 | tf_op jit(solution)/shard_map/while/body/eval_jaxpr/ppermute | solution.py:45
  501.8 11.2 %collective-permute-done.3 = bf16[40,1024]{1,0:T(8,128)(2,1)S(1)} collective-permute-done((bf16[40,1024]{1,0:T(8,128)(2,1)S(1)}, bf16[40,1024]{1,0:T(8,128)(2,1)S(1)}, u32[]{:S(2)}, u32[]{:S(2)}) %collective-permute-start.3) | collective-permute-done | bytes 81952 | tf_op jit(solution)/shard_map/while/body/eval_jaxpr/ppermute | solution.py:55
  544.2 6.1 collective-permute-done.15.refs_2_
  550.6 8.2 %collective-permute-start.17 = (bf16[128,1024]{1,0:T(8,128)(2,1)S(1)}, bf16[128,1024]{1,0:T(8,128)(2,1)S(1)}, u32[]{:S(2)}, u32[]{:S(2)}) collective-permute-start(bf16[128,1024]{1,0:T(8,128)(2,1)S(1)} %get-tuple-element.613), channel_id=1, source_target_pairs={{0,1},{1,0},{2,3},{3,2},{4,5},{5,4},{6,7},{7,6},{8,9},{9,8},{10,11... | collective-permute-start | bytes 786440 | tf_op jit(solution)/shard_map/while/body/eval_jaxpr/ppermute | solution.py:45
  569.1 10.2 %collective-permute-done.3 = bf16[40,1024]{1,0:T(8,128)(2,1)S(1)} collective-permute-done((bf16[40,1024]{1,0:T(8,128)(2,1)S(1)}, bf16[40,1024]{1,0:T(8,128)(2,1)S(1)}, u32[]{:S(2)}, u32[]{:S(2)}) %collective-permute-start.3) | collective-permute-done | bytes 81952 | tf_op jit(solution)/shard_map/while/body/eval_jaxpr/ppermute | solution.py:55
  615.7 8.5 %collective-permute-start.17 = (bf16[128,1024]{1,0:T(8,128)(2,1)S(1)}, bf16[128,1024]{1,0:T(8,128)(2,1)S(1)}, u32[]{:S(2)}, u32[]{:S(2)}) collective-permute-start(bf16[128,1024]{1,0:T(8,128)(2,1)S(1)} %get-tuple-element.613), channel_id=1, source_target_pairs={{0,1},{1,0},{2,3},{3,2},{4,5},{5,4},{6,7},{7,6},{8,9},{9,8},{10,11... | collective-permute-start | bytes 786440 | tf_op jit(solution)/shard_map/while/body/eval_jaxpr/ppermute | solution.py:45
  (450 shorter events, 413.4 us)
Async XLA Ops:
  9.7 41.5 %collective-permute-start.19 = (bf16[384,1024]{1,0:T(8,128)(2,1)}, bf16[384,1024]{1,0:T(8,128)(2,1)S(1)}, u32[]{:S(2)}, u32[]{:S(2)}) collective-permute-start(bf16[384,1024]{1,0:T(8,128)(2,1)} %get-tuple-element.465), channel_id=1, source_target_pairs={{0,8},{8,16},{16,24},{24,0},{1,9},{9,17},{17,25},{25,1},{2,10},{10... | collective-permute-start | bytes 2359304 | tf_op jit(solution)/shard_map/ppermute | solution.py:40
  9.7 41.6 %collective-permute-start.20 = (bf16[384,1024]{1,0:T(8,128)(2,1)}, bf16[384,1024]{1,0:T(8,128)(2,1)}, u32[]{:S(2)}, u32[]{:S(2)}) collective-permute-start(bf16[384,1024]{1,0:T(8,128)(2,1)} %get-tuple-element.467), channel_id=1, source_target_pairs={{0,24},{8,0},{16,8},{24,16},{1,25},{9,1},{17,9},{25,17},{2,26},{10... | collective-permute-start | bytes 2359304 | tf_op jit(solution)/shard_map/ppermute | solution.py:40
  12.5 41.5 %collective-permute-start.21 = (bf16[384,1024]{1,0:T(8,128)(2,1)S(1)}, bf16[384,1024]{1,0:T(8,128)(2,1)S(1)}, u32[]{:S(2)}, u32[]{:S(2)}) collective-permute-start(bf16[384,1024]{1,0:T(8,128)(2,1)S(1)} %get-tuple-element.464), channel_id=1, source_target_pairs={{0,16},{8,24},{16,0},{24,8},{1,17},{9,25},{17,1},{25,9},{2,18},{10... | collective-permute-start | bytes 2359304 | tf_op jit(solution)/shard_map/ppermute | solution.py:40
  28.6 22.1 %collective-permute-start.26 = (bf16[80,1024]{1,0:T(8,128)(2,1)S(1)}, bf16[80,1024]{1,0:T(8,128)(2,1)S(1)}, u32[]{:S(2)}, u32[]{:S(2)}) collective-permute-start(bf16[80,1024]{1,0:T(8,128)(2,1)S(1)} %constant_dynamic-update-slice_fusion.4.refs_4_), channel_id=1, source_target_pairs={{0,8},{8,16},{16,24},{24,0},{1,9},{9,17},{17,25},{25,1},{2,10},{10... | collective-permute-start | bytes 491528 | tf_op jit(solution)/shard_map/ppermute | solution.py:40
  30.1 28.9 %collective-permute-start.28 = (bf16[80,1024]{1,0:T(8,128)(2,1)S(1)}, bf16[80,1024]{1,0:T(8,128)(2,1)S(1)}, u32[]{:S(2)}, u32[]{:S(2)}) collective-permute-start(bf16[80,1024]{1,0:T(8,128)(2,1)S(1)} %constant_dynamic-update-slice_fusion.4.refs_4_), channel_id=1, source_target_pairs={{0,24},{8,0},{16,8},{24,16},{1,25},{9,1},{17,9},{25,17},{2,26},{10... | collective-permute-start | bytes 491528 | tf_op jit(solution)/shard_map/ppermute | solution.py:40
  99.9 35.0 %collective-permute-start.10 = (bf16[128,1024]{1,0:T(8,128)(2,1)S(1)}, bf16[128,1024]{1,0:T(8,128)(2,1)S(1)}, u32[]{:S(2)}, u32[]{:S(2)}) collective-permute-start(bf16[128,1024]{1,0:T(8,128)(2,1)S(1)} %get-tuple-element.637.stream), channel_id=1, source_target_pairs={{0,32},{32,64},{64,96},{96,128},{128,160},{160,192},{192,224},{224... | collective-permute-start | bytes 786440 | tf_op jit(solution)/shard_map/while/body/eval_jaxpr/ppermute | solution.py:40
  102.2 18.8 %collective-permute-start = (bf16[40,1024]{1,0:T(8,128)(2,1)S(1)}, bf16[40,1024]{1,0:T(8,128)(2,1)S(1)}, u32[]{:S(2)}, u32[]{:S(2)}) collective-permute-start(bf16[40,1024]{1,0:T(8,128)(2,1)S(1)} %get-tuple-element.597), channel_id=1, source_target_pairs={{0,36},{1,37},{2,38},{3,39},{4,32},{5,33},{6,34},{7,35},{32,68},{3... | collective-permute-start | bytes 245768 | tf_op jit(solution)/shard_map/while/body/eval_jaxpr/ppermute | solution.py:55
  164.4 38.4 %collective-permute-start.10 = (bf16[128,1024]{1,0:T(8,128)(2,1)S(1)}, bf16[128,1024]{1,0:T(8,128)(2,1)S(1)}, u32[]{:S(2)}, u32[]{:S(2)}) collective-permute-start(bf16[128,1024]{1,0:T(8,128)(2,1)S(1)} %get-tuple-element.637.stream), channel_id=1, source_target_pairs={{0,32},{32,64},{64,96},{96,128},{128,160},{160,192},{192,224},{224... | collective-permute-start | bytes 786440 | tf_op jit(solution)/shard_map/while/body/eval_jaxpr/ppermute | solution.py:40
  164.5 20.3 %collective-permute-start.3 = (bf16[40,1024]{1,0:T(8,128)(2,1)S(1)}, bf16[40,1024]{1,0:T(8,128)(2,1)S(1)}, u32[]{:S(2)}, u32[]{:S(2)}) collective-permute-start(bf16[40,1024]{1,0:T(8,128)(2,1)S(1)} %get-tuple-element.600), channel_id=1, source_target_pairs={{0,32},{1,33},{2,34},{3,35},{4,36},{5,37},{6,38},{7,39},{32,64},{3... | collective-permute-start | bytes 245768 | tf_op jit(solution)/shard_map/while/body/eval_jaxpr/ppermute | solution.py:55
  165.1 22.3 %collective-permute-start = (bf16[40,1024]{1,0:T(8,128)(2,1)S(1)}, bf16[40,1024]{1,0:T(8,128)(2,1)S(1)}, u32[]{:S(2)}, u32[]{:S(2)}) collective-permute-start(bf16[40,1024]{1,0:T(8,128)(2,1)S(1)} %get-tuple-element.597), channel_id=1, source_target_pairs={{0,36},{1,37},{2,38},{3,39},{4,32},{5,33},{6,34},{7,35},{32,68},{3... | collective-permute-start | bytes 245768 | tf_op jit(solution)/shard_map/while/body/eval_jaxpr/ppermute | solution.py:55
  230.2 37.8 %collective-permute-start.10 = (bf16[128,1024]{1,0:T(8,128)(2,1)S(1)}, bf16[128,1024]{1,0:T(8,128)(2,1)S(1)}, u32[]{:S(2)}, u32[]{:S(2)}) collective-permute-start(bf16[128,1024]{1,0:T(8,128)(2,1)S(1)} %get-tuple-element.637.stream), channel_id=1, source_target_pairs={{0,32},{32,64},{64,96},{96,128},{128,160},{160,192},{192,224},{224... | collective-permute-start | bytes 786440 | tf_op jit(solution)/shard_map/while/body/eval_jaxpr/ppermute | solution.py:40
  230.3 20.0 %collective-permute-start.3 = (bf16[40,1024]{1,0:T(8,128)(2,1)S(1)}, bf16[40,1024]{1,0:T(8,128)(2,1)S(1)}, u32[]{:S(2)}, u32[]{:S(2)}) collective-permute-start(bf16[40,1024]{1,0:T(8,128)(2,1)S(1)} %get-tuple-element.600), channel_id=1, source_target_pairs={{0,32},{1,33},{2,34},{3,35},{4,36},{5,37},{6,38},{7,39},{32,64},{3... | collective-permute-start | bytes 245768 | tf_op jit(solution)/shard_map/while/body/eval_jaxpr/ppermute | solution.py:55
  230.6 22.3 %collective-permute-start = (bf16[40,1024]{1,0:T(8,128)(2,1)S(1)}, bf16[40,1024]{1,0:T(8,128)(2,1)S(1)}, u32[]{:S(2)}, u32[]{:S(2)}) collective-permute-start(bf16[40,1024]{1,0:T(8,128)(2,1)S(1)} %get-tuple-element.597), channel_id=1, source_target_pairs={{0,36},{1,37},{2,38},{3,39},{4,32},{5,33},{6,34},{7,35},{32,68},{3... | collective-permute-start | bytes 245768 | tf_op jit(solution)/shard_map/while/body/eval_jaxpr/ppermute | solution.py:55
  296.7 36.0 %collective-permute-start.10 = (bf16[128,1024]{1,0:T(8,128)(2,1)S(1)}, bf16[128,1024]{1,0:T(8,128)(2,1)S(1)}, u32[]{:S(2)}, u32[]{:S(2)}) collective-permute-start(bf16[128,1024]{1,0:T(8,128)(2,1)S(1)} %get-tuple-element.637.stream), channel_id=1, source_target_pairs={{0,32},{32,64},{64,96},{96,128},{128,160},{160,192},{192,224},{224... | collective-permute-start | bytes 786440 | tf_op jit(solution)/shard_map/while/body/eval_jaxpr/ppermute | solution.py:40
  296.9 21.2 %collective-permute-start = (bf16[40,1024]{1,0:T(8,128)(2,1)S(1)}, bf16[40,1024]{1,0:T(8,128)(2,1)S(1)}, u32[]{:S(2)}, u32[]{:S(2)}) collective-permute-start(bf16[40,1024]{1,0:T(8,128)(2,1)S(1)} %get-tuple-element.597), channel_id=1, source_target_pairs={{0,36},{1,37},{2,38},{3,39},{4,32},{5,33},{6,34},{7,35},{32,68},{3... | collective-permute-start | bytes 245768 | tf_op jit(solution)/shard_map/while/body/eval_jaxpr/ppermute | solution.py:55
  362.5 36.0 %collective-permute-start.10 = (bf16[128,1024]{1,0:T(8,128)(2,1)S(1)}, bf16[128,1024]{1,0:T(8,128)(2,1)S(1)}, u32[]{:S(2)}, u32[]{:S(2)}) collective-permute-start(bf16[128,1024]{1,0:T(8,128)(2,1)S(1)} %get-tuple-element.637.stream), channel_id=1, source_target_pairs={{0,32},{32,64},{64,96},{96,128},{128,160},{160,192},{192,224},{224... | collective-permute-start | bytes 786440 | tf_op jit(solution)/shard_map/while/body/eval_jaxpr/ppermute | solution.py:40
  362.7 21.1 %collective-permute-start = (bf16[40,1024]{1,0:T(8,128)(2,1)S(1)}, bf16[40,1024]{1,0:T(8,128)(2,1)S(1)}, u32[]{:S(2)}, u32[]{:S(2)}) collective-permute-start(bf16[40,1024]{1,0:T(8,128)(2,1)S(1)} %get-tuple-element.597), channel_id=1, source_target_pairs={{0,36},{1,37},{2,38},{3,39},{4,32},{5,33},{6,34},{7,35},{32,68},{3... | collective-permute-start | bytes 245768 | tf_op jit(solution)/shard_map/while/body/eval_jaxpr/ppermute | solution.py:55
  428.4 35.9 %collective-permute-start.10 = (bf16[128,1024]{1,0:T(8,128)(2,1)S(1)}, bf16[128,1024]{1,0:T(8,128)(2,1)S(1)}, u32[]{:S(2)}, u32[]{:S(2)}) collective-permute-start(bf16[128,1024]{1,0:T(8,128)(2,1)S(1)} %get-tuple-element.637.stream), channel_id=1, source_target_pairs={{0,32},{32,64},{64,96},{96,128},{128,160},{160,192},{192,224},{224... | collective-permute-start | bytes 786440 | tf_op jit(solution)/shard_map/while/body/eval_jaxpr/ppermute | solution.py:40
  428.6 21.1 %collective-permute-start = (bf16[40,1024]{1,0:T(8,128)(2,1)S(1)}, bf16[40,1024]{1,0:T(8,128)(2,1)S(1)}, u32[]{:S(2)}, u32[]{:S(2)}) collective-permute-start(bf16[40,1024]{1,0:T(8,128)(2,1)S(1)} %get-tuple-element.597), channel_id=1, source_target_pairs={{0,36},{1,37},{2,38},{3,39},{4,32},{5,33},{6,34},{7,35},{32,68},{3... | collective-permute-start | bytes 245768 | tf_op jit(solution)/shard_map/while/body/eval_jaxpr/ppermute | solution.py:55
  494.3 36.0 %collective-permute-start.10 = (bf16[128,1024]{1,0:T(8,128)(2,1)S(1)}, bf16[128,1024]{1,0:T(8,128)(2,1)S(1)}, u32[]{:S(2)}, u32[]{:S(2)}) collective-permute-start(bf16[128,1024]{1,0:T(8,128)(2,1)S(1)} %get-tuple-element.637.stream), channel_id=1, source_target_pairs={{0,32},{32,64},{64,96},{96,128},{128,160},{160,192},{192,224},{224... | collective-permute-start | bytes 786440 | tf_op jit(solution)/shard_map/while/body/eval_jaxpr/ppermute | solution.py:40
  494.4 21.2 %collective-permute-start = (bf16[40,1024]{1,0:T(8,128)(2,1)S(1)}, bf16[40,1024]{1,0:T(8,128)(2,1)S(1)}, u32[]{:S(2)}, u32[]{:S(2)}) collective-permute-start(bf16[40,1024]{1,0:T(8,128)(2,1)S(1)} %get-tuple-element.597), channel_id=1, source_target_pairs={{0,36},{1,37},{2,38},{3,39},{4,32},{5,33},{6,34},{7,35},{32,68},{3... | collective-permute-start | bytes 245768 | tf_op jit(solution)/shard_map/while/body/eval_jaxpr/ppermute | solution.py:55
  560.5 36.1 %collective-permute-start.10 = (bf16[128,1024]{1,0:T(8,128)(2,1)S(1)}, bf16[128,1024]{1,0:T(8,128)(2,1)S(1)}, u32[]{:S(2)}, u32[]{:S(2)}) collective-permute-start(bf16[128,1024]{1,0:T(8,128)(2,1)S(1)} %get-tuple-element.637.stream), channel_id=1, source_target_pairs={{0,32},{32,64},{64,96},{96,128},{128,160},{160,192},{192,224},{224... | collective-permute-start | bytes 786440 | tf_op jit(solution)/shard_map/while/body/eval_jaxpr/ppermute | solution.py:40
  560.6 18.7 %collective-permute-start.3 = (bf16[40,1024]{1,0:T(8,128)(2,1)S(1)}, bf16[40,1024]{1,0:T(8,128)(2,1)S(1)}, u32[]{:S(2)}, u32[]{:S(2)}) collective-permute-start(bf16[40,1024]{1,0:T(8,128)(2,1)S(1)} %get-tuple-element.600), channel_id=1, source_target_pairs={{0,32},{1,33},{2,34},{3,35},{4,36},{5,37},{6,38},{7,39},{32,64},{3... | collective-permute-start | bytes 245768 | tf_op jit(solution)/shard_map/while/body/eval_jaxpr/ppermute | solution.py:55
  560.7 21.3 %collective-permute-start = (bf16[40,1024]{1,0:T(8,128)(2,1)S(1)}, bf16[40,1024]{1,0:T(8,128)(2,1)S(1)}, u32[]{:S(2)}, u32[]{:S(2)}) collective-permute-start(bf16[40,1024]{1,0:T(8,128)(2,1)S(1)} %get-tuple-element.597), channel_id=1, source_target_pairs={{0,36},{1,37},{2,38},{3,39},{4,32},{5,33},{6,34},{7,35},{32,68},{3... | collective-permute-start | bytes 245768 | tf_op jit(solution)/shard_map/while/body/eval_jaxpr/ppermute | solution.py:55
  (147 other events, 1211.5 us)
